TPU v7x, 32 devices: a whole 2x2x4 slice. The times are simulated.
32 devices in a mesh: gx: 4 (over z), gy: 4 (over y, x), gz: 2 (over core).
Axes of the slice: x: 2, y: 2, z: 4, core: 2. Of those that a mesh axis runs over, the one named last changes fastest.
Arguments:
- coarse_field: float32 [3, 128, 128, 512], P(None, 'gx', 'gy', 'gz'), may hold values from -6 to 6
- fine_field: float32 [3, 128, 16, 256], P(None, ('gx', 'gy', 'gz')), may hold values from -6 to 6
- viscosity: float32 [128, 16, 256], P(('gx', 'gy', 'gz')), may hold values from 0.1 to 1
- corners: int32 [64, 3], replicated, may hold values from 0 to 504, as said below
- grid_slot: int32 [64], replicated, may hold values from 0 to 127, as said below
- neighbors: int32 [64, 2], replicated, may hold values from -1 to 63, as said below
Outputs:
- fine_out: float32 [3, 128, 16, 256], P(None, ('gx', 'gy', 'gz'))
- coarse_out: float32 [3, 128, 128, 512], P(None, 'gx', 'gy', 'gz')
Inputs may be any that keep to these rules, and one draw needn't show every extreme that they name: Each box is 8 coarse cells on a side, its corner coordinates are multiples of 8, it lies inside the domain and inside one coarse brick of 32 x 32 x 256 cells, and different grids have different boxes. A brick holds either no box or exactly 4 boxes, which share their y and z corners and are grids of one wake. `grid_slot`: different grids have different slots. A grid's slot lies on a device with the same gz index as the brick that holds its box. Every device holds at most 4 grids, some device holds 4 grids in every draw, and all grids of one device lie in one brick. `neighbors`: entry 0 is the grid of the same wake whose box touches the grid's lower x face, entry 1 the one touching its upper x face, or -1 where there is none.
All inputs are finite; a program needn't handle non-finite values.
Results may differ from a plain program's by a relative error of at most 0.00005.
Values sent between devices are 32-bit elements; how exact they have to be, the bound alone decides.
A program may use at most 128 MiB of HBM per device.

v0:
```python
import functools
import numpy as np
import jax
import jax.numpy as jnp
from jax import lax
from jax.experimental import pallas as pl
from jax.experimental.pallas import tpu as pltpu
from jax.sharding import PartitionSpec as P

B = 8
F = 16
SLOTS = 4
SIDE = B + 2
LANES = 128
MEAN_ROWS = 12
PLANES = 4
PLANE_ROWS = 6
step_rate = 0.15
HIGHEST = lax.Precision.HIGHEST


def up(n, m):
    return -(-n // m) * m


def tables():
    tangent = np.zeros((F, SIDE), np.float32)
    for f in range(F):
        c = f // 2 + 1
        tangent[f, c] = 0.75
        tangent[f, c - 1 if f % 2 == 0 else c + 1] = 0.25
    low = np.zeros((SIDE,), np.float32)
    low[0], low[1] = 0.75, 0.25
    return tangent, low, low[::-1].copy()


def edge_matrices(nx):
    tangent, low, high = tables()
    eye = np.eye(SIDE, dtype=np.float32)
    wide = 4 * SIDE
    cut = np.zeros((SIDE, SIDE, 4, SIDE), np.float32)
    cut[:, :, 0] = np.einsum("b,cd->bcd", low, eye)
    cut[:, :, 1] = np.einsum("b,cd->bcd", high, eye)
    cut[:, :, 2] = np.einsum("bd,c->bcd", eye, low)
    cut[:, :, 3] = np.einsum("bd,c->bcd", eye, high)
    put = np.zeros((4, SIDE, F, F), np.float32)
    put[0, :, 0, :] = tangent.T
    put[1, :, F - 1, :] = tangent.T
    put[2, :, :, 0] = tangent.T
    put[3, :, :, F - 1] = tangent.T
    rows = up(3 * nx, 8)
    edge_rows = up(nx + 6, 8)
    columns = np.zeros((3, LANES, LANES), np.float32)
    places = np.zeros((3, LANES, F * F), np.float32)
    lines = np.zeros((4, edge_rows, rows), np.float32)
    for k in range(3):
        columns[k, : SIDE * SIDE, k * wide : (k + 1) * wide] = cut.reshape(SIDE * SIDE, wide)
        places[k, k * wide : (k + 1) * wide] = put.reshape(wide, F * F)
        lines[k, np.arange(nx), k * nx + np.arange(nx)] = 1.0
        for row, outer, inner in ((0, 0, 1), (1, nx - 1, nx - 2)):
            lines[3, nx + 2 * k + row, k * nx + outer] = 0.75
            lines[3, nx + 2 * k + row, k * nx + inner] = 0.25
    across = np.zeros((LANES, F * F), np.float32)
    across[: SIDE * SIDE] = np.einsum("sb,tc->bcst", tangent, tangent).reshape(SIDE * SIDE, F * F)
    return columns, lines, places, across


def mean_matrices():
    lanes = np.zeros((F * F, LANES), np.float32)
    for y in range(F):
        for z in range(F):
            for half in range(2):
                lanes[y * F + z, half * 64 + (y // 2) * B + z // 2] = 0.125
    rows = np.zeros((2, SLOTS * MEAN_ROWS, 3 * SLOTS * F), np.float32)
    for half in range(2):
        for s in range(SLOTS):
            for k in range(3):
                for a in range(B // 2):
                    for p in range(2):
                        x = 2 * (half * (B // 2) + a) + p
                        rows[half, s * MEAN_ROWS + k * (B // 2) + a, (k * SLOTS + s) * F + x] = 1.0
    return lanes, rows


def dot(a, b):
    return jnp.dot(a, b, precision=HIGHEST, preferred_element_type=jnp.float32)


def edge_kernel(chosen, slab, fine, columns, lines, edges, planes):
    total = dot(lines[3], slab[...])
    for k in range(3):
        total += dot(lines[k], dot(slab[...], columns[k]))
    edges[...] = total
    for p in range(PLANES):
        slot = chosen[p] // 2
        low_side = chosen[p] % 2 == 0
        for k in range(3):
            v = fine[k, slot]
            line = jnp.where(low_side, v[F - 1 : F], v[0:1])
            for h in range(2):
                at = p * PLANE_ROWS + k * 2 + h
                planes[at : at + 1] = line[:, h * LANES : (h + 1) * LANES]


def fine_kernel(
    nx, ny, width, flags, edges, planes, fine, visc, places, across, lane_mean, row_mean,
    fine_out, picked, slabs, plane_buf, mean_send, means, advs, send_sem, recv_sem, own_sem,
):
    count = nx * ny
    me = lax.axis_index("gx") * ny + lax.axis_index("gy")

    def peer(o):
        t = lax.rem(me + o, count)
        return {"gx": t // ny, "gy": lax.rem(t, ny)}

    def remote(o, which, src, dst):
        return pltpu.make_async_remote_copy(
            src_ref=src, dst_ref=dst, send_sem=send_sem.at[which, o], recv_sem=recv_sem.at[which, o],
            device_id=peer(o), device_id_type=pl.DeviceIdType.MESH,
        )

    def slab_copy(o):
        return remote(o, 0, edges, slabs.at[me])

    def plane_copy(o):
        return remote(o, 1, planes, plane_buf.at[me])

    def mean_copy(o):
        return remote(o, 2, mean_send, means.at[me])

    barrier = pltpu.get_barrier_semaphore()

    def greet(o, c):
        pl.semaphore_signal(barrier, inc=1, device_id=peer(o), device_id_type=pl.DeviceIdType.MESH)
        return c

    lax.fori_loop(1, count, greet, 0)
    own_slab = pltpu.make_async_copy(edges, slabs.at[me], own_sem.at[0])
    own_plane = pltpu.make_async_copy(planes, plane_buf.at[me], own_sem.at[1])
    own_slab.start()
    own_plane.start()
    pl.semaphore_wait(barrier, count - 1)

    def send_slab(o, c):
        slab_copy(o).start()
        return c

    def send_plane(o, c):
        plane_copy(o).start()
        return c

    lax.fori_loop(1, count, send_slab, 0)
    lax.fori_loop(1, count, send_plane, 0)
    own_slab.wait()
    own_plane.wait()

    def finish_slab(o, c):
        slab_copy(o).wait()
        return c

    def finish_plane(o, c):
        plane_copy(o).wait()
        return c

    lax.fori_loop(1, count, finish_slab, 0)

    def flag(group, s):
        return flags[1 + group * SLOTS + s]

    mine = slabs[flags[0]]
    shape = (SLOTS * F, mine.shape[0])
    line_id = lax.broadcasted_iota(jnp.int32, shape, 0)
    from_row = lax.broadcasted_iota(jnp.int32, shape, 1)
    box = jnp.full(shape, flag(1, 0), jnp.int32)
    for s in range(1, SLOTS):
        box = jnp.where(line_id // F == s, flag(1, s), box)
    i_id = line_id % F
    center = B * box + i_id // 2 + 1
    other = jnp.where(i_id % 2 == 0, center - 1, center + 1)
    blend = jnp.where(from_row == center, 0.75, jnp.where(from_row == other, 0.25, 0.0))
    along = dot(blend, mine)
    ghosts = [dot(along, places[k]) for k in range(3)]
    xface = dot(mine, across[...])[width : width + 6]
    lax.fori_loop(1, count, finish_plane, 0)
    lane = lax.broadcasted_iota(jnp.int32, (F, F * F), 1)
    row = lax.broadcasted_iota(jnp.int32, (F, F * F), 0)
    lz = lane % F
    for s in range(SLOTS):
        active = flag(0, s) > 0
        near = []
        for side in range(2):
            base = 2 + 5 * side
            far = plane_buf[flag(base, s)]
            rank = flag(base + 1, s)
            chosen = far[:PLANE_ROWS]
            for p in range(1, PLANES):
                chosen = jnp.where(rank == p, far[p * PLANE_ROWS : (p + 1) * PLANE_ROWS], chosen)
            near.append((chosen, flag(base + 2, s), flag(base + 3, s) > 0, flag(base + 4, s) > 0))
        for k in range(3):
            v = fine[k, s]
            ends = []
            for side in range(2):
                chosen, slot, local, has = near[side]
                x = (F - 1) * (1 - side)
                far = jnp.concatenate([chosen[2 * k : 2 * k + 1], chosen[2 * k + 1 : 2 * k + 2]], axis=1)
                here = fine[k, slot][x : x + 1]
                outer = xface[2 * k + side : 2 * k + side + 1]
                ends.append(jnp.where(has, jnp.where(local, here, far), outer))
            lower, upper = ends
            total = jnp.where(row == 0, lower, pltpu.roll(v, 1, 0))
            total += jnp.where(row == F - 1, upper, pltpu.roll(v, F - 1, 0))
            total += jnp.where(lane < F, 0.0, pltpu.roll(v, F, 1))
            total += jnp.where(lane >= F * F - F, 0.0, pltpu.roll(v, F * F - F, 1))
            total += jnp.where(lz == 0, 0.0, pltpu.roll(v, 1, 1))
            total += jnp.where(lz == F - 1, 0.0, pltpu.roll(v, F * F - 1, 1))
            at = (k * SLOTS + s) * F
            total += ghosts[k][s * F : s * F + F] - 6.0 * v
            adv = v + step_rate * visc[s] * total
            advs[at : at + F] = adv
            fine_out[k, s] = jnp.where(active, adv, 0.0)
    z = dot(advs[...], lane_mean[...])
    first = dot(row_mean[0], z)
    second = dot(row_mean[1], z)
    lane_m = lax.broadcasted_iota(jnp.int32, first.shape, 1)
    packed = jnp.where(lane_m < 64, first, second)
    mean_send[...] = packed
    means[me] = packed

    def send_mean(o, c):
        mean_copy(o).start()
        return c

    lax.fori_loop(1, count, send_mean, 0)

    def finish_mean(o, c):
        mean_copy(o).wait()
        return c

    lax.fori_loop(1, count, finish_mean, 0)
    for s in range(SLOTS):
        got = means[flag(12, s)]
        part = flag(13, s)
        value = got[:MEAN_ROWS]
        for p in range(1, SLOTS):
            value = jnp.where(part == p, got[p * MEAN_ROWS : (p + 1) * MEAN_ROWS], value)
        picked[s] = value


def plan_kernel(ny, nz, bricks, corners, grid_slot, neighbors, flags, at, chosen, held):
    ix, iy, iz = lax.axis_index("gx"), lax.axis_index("gy"), lax.axis_index("gz")
    device = (ix * ny + iy) * nz + iz
    total = held.shape[0]

    def put(group, s, value):
        flags[1 + group * SLOTS + s] = value

    def clear(i, c):
        for j in range(8):
            held[i * 8 + j] = -1
        return c

    lax.fori_loop(0, total // 8, clear, 0)
    for s in range(SLOTS):
        put(12, s, 0)
        put(13, s, 0)
        chosen[s] = 0
    for i in range(3):
        at[i] = 0

    def scan(g, c):
        held[grid_slot[g]] = g
        x, y, z = corners[0, g], corners[1, g], corners[2, g]
        mine = (x // bricks[0] == ix) & (y // bricks[1] == iy) & (z // bricks[2] == iz)

        @pl.when(mine)
        def _():
            box = lax.rem(x, bricks[0]) // B
            flags[1 + 12 * SLOTS + box] = grid_slot[g] // (SLOTS * nz)
            flags[1 + 13 * SLOTS + box] = lax.rem(grid_slot[g], SLOTS)
            at[0] = lax.rem(y, bricks[1])
            at[1] = lax.rem(z, bricks[2])
            at[2] = 1

        return c

    lax.fori_loop(0, grid_slot.shape[0], scan, 0)

    def leaves(n, side):
        grid = held[n]
        near = neighbors[1 - side, jnp.maximum(grid, 0)]
        other = grid_slot[jnp.maximum(near, 0)] // SLOTS
        return jnp.where((grid >= 0) & (near >= 0) & (other != n // SLOTS), 1, 0)

    def rank_of(n, side):
        first = n // SLOTS * SLOTS
        rank = 0 if side == 0 else leaves(n, 0)
        for s in range(SLOTS):
            both = leaves(first + s, 0) + leaves(first + s, 1)
            rank = rank + jnp.where(first + s < n, both, 0)
        return rank

    home = jnp.int32(0)
    count = jnp.int32(0)
    for s in range(SLOTS):
        n = device * SLOTS + s
        grid = held[n]
        active = grid >= 0
        g = jnp.maximum(grid, 0)
        put(0, s, jnp.where(active, 1, 0))
        put(1, s, jnp.where(active, lax.rem(corners[0, g], bricks[0]) // B, 0))
        here = corners[0, g] // bricks[0] * ny + corners[1, g] // bricks[1]
        home = jnp.where(active, here, home)
        for side in range(2):
            base = 2 + 5 * side
            near = neighbors[side, g]
            m = grid_slot[jnp.maximum(near, 0)]
            put(base, s, m // (SLOTS * nz))
            put(base + 1, s, rank_of(m, side))
            put(base + 2, s, lax.rem(m, SLOTS))
            put(base + 3, s, jnp.where(m // SLOTS == device, 1, 0))
            put(base + 4, s, jnp.where(active & (near >= 0), 1, 0))
        for side in range(2):
            out = leaves(n, side)

            @pl.when(out > 0)
            def _():
                chosen[count] = s * 2 + side

            count = count + out
    flags[0] = home


def coarse_kernel(at, field, rows, out):
    n = field.shape[0]
    out[...] = field[...]
    y = pl.multiple_of(at[0], B)
    z = at[1]
    r3 = lax.broadcast_in_dim(rows[...], (n, B, B * B), (0, 2))
    sub = lax.broadcasted_iota(jnp.int32, r3.shape, 1)
    ln = lax.broadcasted_iota(jnp.int32, r3.shape, 2)
    spread = jnp.where(ln // B == sub, r3, 0.0).reshape(n * B, B * B)
    width = field.shape[2]
    c_id = lax.broadcasted_iota(jnp.int32, (B * B, width), 0) % B
    z_id = lax.broadcasted_iota(jnp.int32, (B * B, width), 1)
    place = jnp.where(z_id == z + c_id, 1.0, 0.0)
    value = dot(spread, place).reshape(n, B, width)
    z3 = lax.broadcasted_iota(jnp.int32, value.shape, 2)
    inside = (z3 >= z) & (z3 < z + B) & (at[2] > 0)
    out[:, pl.ds(y, B), :] = jnp.where(inside, value, field[:, pl.ds(y, B), :])


def shift(low_part, high_part, axis):
    count = lax.axis_size(axis)
    low = lax.ppermute(high_part, axis, [(i, i + 1) for i in range(count - 1)])
    high = lax.ppermute(low_part, axis, [(i + 1, i) for i in range(count - 1)])
    return low, high


def cut_slab(field, y, z):
    nx, ny, nz = field.shape[1:]
    if lax.axis_size("gz") == 2:
        upper = lax.axis_index("gz") == 1
        other = lax.ppermute(jnp.where(upper, field[..., :1], field[..., -1:]), "gz", [(0, 1), (1, 0)])
        zlo, zhi = jnp.where(upper, other, 0.0), jnp.where(upper, 0.0, other)
    else:
        zlo, zhi = shift(field[..., :1], field[..., -1:], "gz")

    def wide(part, lo, hi):
        return jnp.concatenate([lo, part, hi], axis=3)

    first = wide(field[:, :1], zlo[:, :1], zhi[:, :1])
    last = wide(field[:, -1:], zlo[:, -1:], zhi[:, -1:])
    xlo, xhi = shift(first, last, "gx")

    def line(start, size):
        def cut(a):
            return lax.dynamic_slice_in_dim(a, start, size, axis=2)

        return jnp.concatenate([cut(xlo), wide(cut(field), cut(zlo), cut(zhi)), cut(xhi)], axis=1)

    ylo, yhi = shift(line(0, 1), line(ny - 1, 1), "gy")

    def zcut(a):
        return lax.dynamic_slice_in_dim(a, z, SIDE, axis=3)

    low = jnp.where(y == 0, zcut(ylo), zcut(line(jnp.maximum(y - 1, 0), 1)))
    high = jnp.where(y == ny - B, zcut(yhi), zcut(line(jnp.minimum(y + B, ny - 1), 1)))
    slab = jnp.concatenate([low, zcut(line(y, B)), high], axis=2)
    slab = slab.reshape(3 * (nx + 2), SIDE * SIDE)
    rows = up(3 * (nx + 2), 8)
    return jnp.pad(slab, ((0, rows - 3 * (nx + 2)), (0, LANES - SIDE * SIDE)))


def on_device(coarse_field, fine_field, viscosity, corners, grid_slot, neighbors):
    count_x = lax.axis_size("gx")
    count_y = lax.axis_size("gy")
    count_z = lax.axis_size("gz")
    count = count_x * count_y
    brick_x, brick_y, brick_z = coarse_field.shape[1:]
    smem = pl.BlockSpec(memory_space=pltpu.SMEM)
    flags, at, chosen = pl.pallas_call(
        functools.partial(plan_kernel, count_y, count_z, (brick_x, brick_y, brick_z)),
        out_shape=(
            jax.ShapeDtypeStruct((1 + 14 * SLOTS,), jnp.int32),
            jax.ShapeDtypeStruct((3,), jnp.int32),
            jax.ShapeDtypeStruct((PLANES,), jnp.int32),
        ),
        in_specs=[smem] * 3,
        out_specs=(smem, smem, smem),
        scratch_shapes=[pltpu.SMEM((count * count_z * SLOTS,), jnp.int32)],
        name="plan",
    )(corners.T, grid_slot, neighbors.T)
    anchor_y, anchor_z = at[0], at[1]

    slab = cut_slab(coarse_field, anchor_y, anchor_z)
    columns, lines, places, across = edge_matrices(brick_x + 2)
    edge_rows = lines.shape[1]
    vmem = pl.BlockSpec(memory_space=pltpu.VMEM)
    edges, planes = pl.pallas_call(
        edge_kernel,
        out_shape=(
            jax.ShapeDtypeStruct((edge_rows, LANES), jnp.float32),
            jax.ShapeDtypeStruct((PLANES * PLANE_ROWS, LANES), jnp.float32),
        ),
        in_specs=[smem] + [vmem] * 4,
        out_specs=(vmem, vmem),
        name="edge_cut",
    )(chosen, slab, fine_field, jnp.asarray(columns), jnp.asarray(lines))

    lane_mean, row_mean = mean_matrices()
    fine_out, picked = pl.pallas_call(
        functools.partial(fine_kernel, count_x, count_y, brick_x + 2),
        out_shape=(
            jax.ShapeDtypeStruct(fine_field.shape, jnp.float32),
            jax.ShapeDtypeStruct((SLOTS, MEAN_ROWS, LANES), jnp.float32),
        ),
        in_specs=[smem] + [vmem] * 8,
        out_specs=(vmem, vmem),
        scratch_shapes=[
            pltpu.VMEM((count, edge_rows, LANES), jnp.float32),
            pltpu.VMEM((count, PLANES * PLANE_ROWS, LANES), jnp.float32),
            pltpu.VMEM((SLOTS * MEAN_ROWS, LANES), jnp.float32),
            pltpu.VMEM((count, SLOTS * MEAN_ROWS, LANES), jnp.float32),
            pltpu.VMEM((3 * SLOTS * F, F * F), jnp.float32),
            pltpu.SemaphoreType.DMA((3, count)),
            pltpu.SemaphoreType.DMA((3, count)),
            pltpu.SemaphoreType.DMA((2,)),
        ],
        compiler_params=pltpu.CompilerParams(collective_id=0, has_side_effects=True),
        name="fine_step",
    )(
        flags, edges, planes, fine_field, viscosity, jnp.asarray(places), jnp.asarray(across),
        jnp.asarray(lane_mean), jnp.asarray(row_mean),
    )
    rows = picked[:, : 3 * (B // 2)].reshape(SLOTS, 3, B // 2, 2, B * B)
    rows = rows.transpose(1, 0, 3, 2, 4).reshape(3 * brick_x, B * B)
    block = 16
    coarse_out = pl.pallas_call(
        coarse_kernel,
        out_shape=jax.ShapeDtypeStruct((3 * brick_x, brick_y, brick_z), jnp.float32),
        grid_spec=pltpu.PrefetchScalarGridSpec(
            num_scalar_prefetch=1,
            grid=(3 * brick_x // block,),
            in_specs=[
                pl.BlockSpec((block, brick_y, brick_z), lambda i, at: (i, 0, 0)),
                pl.BlockSpec((block, B * B), lambda i, at: (i, 0)),
            ],
            out_specs=pl.BlockSpec((block, brick_y, brick_z), lambda i, at: (i, 0, 0)),
        ),
        name="coarse_fill",
    )(at, coarse_field.reshape(3 * brick_x, brick_y, brick_z), rows)
    return fine_out, coarse_out.reshape(coarse_field.shape)


def solution(mesh):
    in_specs = (
        P(None, "gx", "gy", "gz"),
        P(None, ("gx", "gy", "gz"), None, None),
        P(("gx", "gy", "gz"), None, None),
        P(),
        P(),
        P(),
    )
    out_specs = (P(None, ("gx", "gy", "gz"), None, None), P(None, "gx", "gy", "gz"))
    return jax.shard_map(
        on_device, mesh=mesh, in_specs=in_specs, out_specs=out_specs, check_vma=False
    )
```

profile of v0, /device:TPU:0, one launch (start us, length us, event | category | flops | bytes accessed | tf_op | source)
XLA Modules:
  0.0 87.2 jit_solution(11695273669293670969)
XLA Ops:
  0.6 2.5 %fusion.20 = (f32[3,32,32,1]{3,2,1,0:T(8,128)S(1)}, f32[3,32,32,1]{3,2,1,0:T(8,128)S(1)}) fusion(f32[3,32,32,256]{3,2,1,0:T(8,128)} %param.12), kind=kLoop, calls=%fused_computation.66 | loop fusion | bytes 49152 | tf_op jit(solution)/shard_map/slice | solution.py:363
  3.1 0.6 copy.120
  3.7 0.6 copy.121
  4.4 0.6 collective-permute-start
  4.9 1.0 %fusion.19 = (f32[3,1,32,256]{3,2,1,0:T(8,128)S(1)}, f32[3,1,32,256]{3,2,1,0:T(8,128)S(1)}) fusion(f32[3,32,32,256]{3,2,1,0:T(8,128)} %param.12), kind=kLoop, calls=%fused_computation.65 | loop fusion | bytes 393216 | tf_op jit(solution)/shard_map/slice | solution.py:371
  5.9 4.7 %plan.1 = (s32[57]{0:T(128)}, s32[3]{0:T(128)}, s32[4]{0:T(128)}) custom-call(s32[3,64]{1,0:T(4,128)} %bitcast.46, s32[64]{0:T(128)} %grid_slot.1, s32[2,64]{1,0:T(2,128)} %bitcast.47), custom_call_target="tpu_custom_call" | custom-call | tf_op jit(solution)/shard_map/plan/pallas_call | solution.py:401
  10.6 1.3 %fusion.23 = (s32[1]{0:T(128)}, s32[1]{0:T(128)}) fusion(s32[3]{0:T(128)} %get-tuple-element.11.at), kind=kLoop, calls=%fused_computation.69 | loop fusion | bytes 16 | tf_op jit(solution)/shard_map/slice | solution.py:413
  14.6 2.2 %fusion.18 = (f32[3,32,1,256]{3,2,1,0:T(1,128)S(1)}, f32[3,32,1,256]{3,2,1,0:T(1,128)S(1)}, f32[3,32,1,256]{3,2,1,0:T(1,128)S(1)}, f32[3,32,1,256]{3,2,1,0:T(1,128)S(1)}) fusion(f32[3,32,32,256]{3,2,1,0:T(8,128)} %param.12, s32[]{:T(128)S(6)} %max.3, s32[]{:T(128)S(6)} %select_n.69), kind=kLoop, calls=%fused_computation.64 | loop fusion | bytes 786440 | tf_op jit(solution)/shard_map/dynamic_slice | solution.py:377
  17.4 1.5 %constant_dynamic-slice_fusion.4 = f32[3,32,8,256]{3,2,1,0:T(8,128)S(1)} fusion(f32[3,32,32,256]{3,2,1,0:T(8,128)} %param.12, s32[]{:T(128)S(6)} %select_n.67), kind=kLoop, calls=%fused_computation.49 | loop fusion | bytes 1572868 | tf_op jit(solution)/shard_map/dynamic_slice | solution.py:377
  22.2 0.0 collective-permute-done
  22.3 0.1 slice_bitcast_fusion.2
  22.4 0.1 copy.88
  22.5 0.1 copy.87
  22.6 0.1 pad_maximum_fusion.3
  22.8 4.5 %collective-permute-start.1 = (f32[3,1,32,258]{3,2,1,0:T(8,128)S(1)}, f32[3,1,32,258]{3,2,1,0:T(8,128)S(1)}, u32[]{:S(2)}, u32[]{:S(2)}) collective-permute-start(f32[3,1,32,258]{3,2,1,0:T(8,128)S(1)} %pad_maximum_fusion.3), channel_id=1, source_target_pairs={{0,8},{8,16},{16,24},{1,9},{9,17},{17,25},{2,10},{10,18},{18,26},{... | collective-permute-start | bytes 297224 | tf_op jit(solution)/shard_map/ppermute | solution.py:354
  27.3 0.1 copy.93
  27.4 0.1 copy.92
  27.5 0.1 pad_maximum_fusion.4
  27.6 1.3 %collective-permute-start.2 = (f32[3,1,32,258]{3,2,1,0:T(8,128)S(1)}, f32[3,1,32,258]{3,2,1,0:T(8,128)S(1)}, u32[]{:S(2)}, u32[]{:S(2)}) collective-permute-start(f32[3,1,32,258]{3,2,1,0:T(8,128)S(1)} %pad_maximum_fusion.4), channel_id=1, source_target_pairs={{8,0},{16,8},{24,16},{9,1},{17,9},{25,17},{10,2},{18,10},{26,18},{... | collective-permute-start | bytes 297224 | tf_op jit(solution)/shard_map/ppermute | solution.py:355
  28.9 0.1 constant_dynamic-slice_fusion.3
  29.0 0.6 copy.101
  29.6 0.6 copy.102
  30.2 0.6 collective-permute-done.1
  30.8 4.4 %collective-permute-done.2 = f32[3,1,32,258]{3,2,1,0:T(8,128)S(1)} collective-permute-done((f32[3,1,32,258]{3,2,1,0:T(8,128)S(1)}, f32[3,1,32,258]{3,2,1,0:T(8,128)S(1)}, u32[]{:S(2)}, u32[]{:S(2)}) %collective-permute-start.2) | collective-permute-done | bytes 99104 | tf_op jit(solution)/shard_map/ppermute | solution.py:355
  35.3 0.1 pad_maximum_fusion.2
  35.4 1.3 %collective-permute-start.4 = (f32[3,34,1,258]{3,1,2,0:T(8,128)S(1)}, f32[3,34,1,258]{3,1,2,0:T(8,128)S(1)}, u32[]{:S(2)}, u32[]{:S(2)}) collective-permute-start(f32[3,34,1,258]{3,1,2,0:T(8,128)S(1)} %pad_maximum_fusion.2), channel_id=1, source_target_pairs={{2,0},{4,2},{6,4},{3,1},{5,3},{7,5},{10,8},{12,10},{14,12},{11,9},... | collective-permute-start | bytes 315800 | tf_op jit(solution)/shard_map/ppermute | solution.py:355
  36.7 0.1 pad_maximum_fusion.1
  36.8 4.6 %collective-permute-start.3 = (f32[3,34,1,258]{3,1,2,0:T(8,128)S(1)}, f32[3,34,1,258]{3,1,2,0:T(8,128)S(1)}, u32[]{:S(2)}, u32[]{:S(2)}) collective-permute-start(f32[3,34,1,258]{3,1,2,0:T(8,128)S(1)} %pad_maximum_fusion.1), channel_id=1, source_target_pairs={{0,2},{2,4},{4,6},{1,3},{3,5},{5,7},{8,10},{10,12},{12,14},{9,11},... | collective-permute-start | bytes 315800 | tf_op jit(solution)/shard_map/ppermute | solution.py:354
  41.4 0.5 fusion.1
  41.9 1.2 %collective-permute-done.4 = f32[3,34,1,258]{3,1,2,0:T(8,128)S(1)} collective-permute-done((f32[3,34,1,258]{3,1,2,0:T(8,128)S(1)}, f32[3,34,1,258]{3,1,2,0:T(8,128)S(1)}, u32[]{:S(2)}, u32[]{:S(2)}) %collective-permute-start.4) | collective-permute-done | bytes 105296 | tf_op jit(solution)/shard_map/ppermute | solution.py:355
  43.1 0.2 fusion.6
  43.3 0.1 copy.114
  43.4 1.1 %collective-permute-done.3 = f32[3,34,1,258]{3,1,2,0:T(8,128)S(1)} collective-permute-done((f32[3,34,1,258]{3,1,2,0:T(8,128)S(1)}, f32[3,34,1,258]{3,1,2,0:T(8,128)S(1)}, u32[]{:S(2)}, u32[]{:S(2)}) %collective-permute-start.3) | collective-permute-done | bytes 105296 | tf_op jit(solution)/shard_map/ppermute | solution.py:354
  44.5 0.2 fusion.11
  44.6 0.1 copy.113
  44.7 0.2 pad_maximum_fusion
  44.9 0.3 reshape.24
  45.2 0.6 pad.4.slab
  45.8 2.7 %edge_cut.1 = (f32[40,128]{1,0:T(8,128)}, f32[24,128]{1,0:T(8,128)}) custom-call(s32[4]{0:T(128)} %get-tuple-element.10.chosen, f32[104,128]{1,0:T(8,128)} %pad.4.slab, f32[3,4,16,256]{3,2,1,0:T(8,128)} %fine.3, f32[3,128,128]{2,1,0:T(8,128)} %constant.36.clone.columns, f32[4,40,104]{2,1,0:T(8,128)} %constant.37.clone.lines), custom_call_target="tpu_custom_call" | custom-call | tf_op jit(solution)/shard_map/edge_cut/pallas_call | solution.py:419
  48.4 29.9 %fine_step.1 = (f32[3,4,16,256]{3,2,1,0:T(8,128)}, f32[4,12,128]{2,1,0:T(8,128)}) custom-call(s32[57]{0:T(128)} %get-tuple-element.9.flags, f32[40,128]{1,0:T(8,128)} %get-tuple-element.12.edges, f32[24,128]{1,0:T(8,128)} %get-tuple-element.13.planes, f32[3,4,16,256]{3,2,1,0:T(8,128)} %fine.3, f32[4,16,256]{2,1,0:T(8,128)} %visc.1, ...), custom_call_target="tpu_custom_call" | custom-call | tf_op jit(solution)/shard_map/fine_step/pallas_call | solution.py:431
  78.3 0.8 copy.117
  79.1 0.1 reshape.21
  79.2 0.6 copy.118
  79.8 0.0 copy-start
  79.8 6.7 %coarse_fill.1 = f32[96,32,256]{2,1,0:T(8,128)} custom-call(s32[3]{0:T(128)} %get-tuple-element.11.at, f32[96,32,256]{2,1,0:T(8,128)} %bitcast.42, f32[96,64]{1,0:T(8,128)} %bitcast.44), custom_call_target="tpu_custom_call" | custom-call | tf_op jit(solution)/shard_map/coarse_fill/pallas_call | solution.py:458
  86.5 0.0 copy-done
  86.5 0.7 copy.127
  (11 shorter events, 0.1 us)
Async XLA Ops:
  4.4 17.9 %collective-permute-start = (f32[3,32,32,1]{2,1,3,0:T(8,128)S(1)}, f32[3,32,32,1]{2,1,3,0:T(8,128)S(1)}, u32[]{:S(2)}, u32[]{:S(2)}) collective-permute-start(f32[3,32,32,1]{2,1,3,0:T(8,128)S(1)} %broadcast_select_fusion.2), channel_id=1, source_target_pairs={{0,1},{1,0},{2,3},{3,2},{4,5},{5,4},{6,7},{7,6},{8,9},{9,8},{10,11... | collective-permute-start | bytes 36872 | tf_op jit(solution)/shard_map/ppermute | solution.py:363
  22.8 8.0 %collective-permute-start.1 = (f32[3,1,32,258]{3,2,1,0:T(8,128)S(1)}, f32[3,1,32,258]{3,2,1,0:T(8,128)S(1)}, u32[]{:S(2)}, u32[]{:S(2)}) collective-permute-start(f32[3,1,32,258]{3,2,1,0:T(8,128)S(1)} %pad_maximum_fusion.3), channel_id=1, source_target_pairs={{0,8},{8,16},{16,24},{1,9},{9,17},{17,25},{2,10},{10,18},{18,26},{... | collective-permute-start | bytes 297224 | tf_op jit(solution)/shard_map/ppermute | solution.py:354
  27.6 7.7 %collective-permute-start.2 = (f32[3,1,32,258]{3,2,1,0:T(8,128)S(1)}, f32[3,1,32,258]{3,2,1,0:T(8,128)S(1)}, u32[]{:S(2)}, u32[]{:S(2)}) collective-permute-start(f32[3,1,32,258]{3,2,1,0:T(8,128)S(1)} %pad_maximum_fusion.4), channel_id=1, source_target_pairs={{8,0},{16,8},{24,16},{9,1},{17,9},{25,17},{10,2},{18,10},{26,18},{... | collective-permute-start | bytes 297224 | tf_op jit(solution)/shard_map/ppermute | solution.py:355
  35.4 7.7 %collective-permute-start.4 = (f32[3,34,1,258]{3,1,2,0:T(8,128)S(1)}, f32[3,34,1,258]{3,1,2,0:T(8,128)S(1)}, u32[]{:S(2)}, u32[]{:S(2)}) collective-permute-start(f32[3,34,1,258]{3,1,2,0:T(8,128)S(1)} %pad_maximum_fusion.2), channel_id=1, source_target_pairs={{2,0},{4,2},{6,4},{3,1},{5,3},{7,5},{10,8},{12,10},{14,12},{11,9},... | collective-permute-start | bytes 315800 | tf_op jit(solution)/shard_map/ppermute | solution.py:355
  36.8 7.6 %collective-permute-start.3 = (f32[3,34,1,258]{3,1,2,0:T(8,128)S(1)}, f32[3,34,1,258]{3,1,2,0:T(8,128)S(1)}, u32[]{:S(2)}, u32[]{:S(2)}) collective-permute-start(f32[3,34,1,258]{3,1,2,0:T(8,128)S(1)} %pad_maximum_fusion.1), channel_id=1, source_target_pairs={{0,2},{2,4},{4,6},{1,3},{3,5},{5,7},{8,10},{10,12},{12,14},{9,11},... | collective-permute-start | bytes 315800 | tf_op jit(solution)/shard_map/ppermute | solution.py:354
  79.8 6.7 %copy-start = (f32[3,4,16,256]{3,2,1,0:T(8,128)S(1)}, f32[3,4,16,256]{3,2,1,0:T(8,128)}, u32[]{:S(2)}) copy-start(f32[3,4,16,256]{3,2,1,0:T(8,128)} %get-tuple-element.58) | copy-start | bytes 589828
where the time goes:
time: 88.3 us; the launch traced here: 87.2 us
  Pallas kernels  43.9 us (50%)
  local copies, waits for them, and re-layouts  14.9 us (17%)
  starting transfers between devices  12.2 us (14%)
  between operations  7.38 us (8%)
  waiting for transfers between devices  7.26 us (8%)
  other arithmetic  1.52 us (2%)
    pallas_call x1, Pallas kernels, on_device(): pl.pallas_call(functools.partial(fine_kernel, count_x, count_y, brick_x +...  29.9 us
    ppermute x2, starting transfers between devices, shift(): low = lax.ppermute(high_part, axis, [(i, i + 1) for i in range(count - 1)])  9.05 us
    pallas_call x1, Pallas kernels, on_device(): pl.pallas_call(coarse_kernel, out_shape=jax.ShapeDtypeStruct((3 * brick_x...  6.67 us
    ppermute x2, waiting for transfers between devices, shift(): high = lax.ppermute(low_part, axis, [(i + 1, i) for i in range(count - 1)])  5.61 us
    dynamic_slice x10, local copies, waits for them, and re-layouts, cut(): return lax.dynamic_slice_in_dim(a, start, size, axis=2)  5.26 us
    pallas_call x1, Pallas kernels, on_device(): pl.pallas_call(functools.partial(plan_kernel, count_y, count_z, (brick_x,...  4.74 us
    pallas_call x1, Pallas kernels, on_device(): pl.pallas_call(edge_kernel, out_shape=(jax.ShapeDtypeStruct((edge_rows, L...  2.65 us
    ppermute x2, starting transfers between devices, shift(): high = lax.ppermute(low_part, axis, [(i + 1, i) for i in range(count - 1)])  2.58 us
  transfers between devices with their start and end apart: 5, of which 4 were waited for; matrix products, arithmetic and copies ran while one was open for 10% of the time, Pallas kernels for 5%

commit v1 on v0

v1 whole, which is shorter than its diff:
```python
import functools
import numpy as np
import jax
import jax.numpy as jnp
from jax import lax
from jax.experimental import pallas as pl
from jax.experimental.pallas import tpu as pltpu
from jax.sharding import PartitionSpec as P

B = 8
F = 16
SLOTS = 4
SIDE = B + 2
LANES = 128
WIDE = 4 * SIDE
IFACES = SLOTS + 1
PLANE_ROWS = 16
A_ROWS = 48
Y_ROWS = 24
E_ROWS = 40
MEAN_ROWS = 12
step_rate = 0.15
MIB = 1 << 20


def tables():
    tangent = np.zeros((F, SIDE), np.float32)
    for f in range(F):
        c = f // 2 + 1
        tangent[f, c] = 0.75
        tangent[f, c - 1 if f % 2 == 0 else c + 1] = 0.25
    low = np.zeros((SIDE,), np.float32)
    low[0], low[1] = 0.75, 0.25
    return tangent, low, low[::-1].copy()


def matrices():
    tangent, low, high = tables()
    eye = np.eye(SIDE, dtype=np.float32)
    cut = np.zeros((SIDE, SIDE, 4, SIDE), np.float32)
    cut[:, :, 0] = np.einsum("b,cd->bcd", low, eye)
    cut[:, :, 1] = np.einsum("b,cd->bcd", high, eye)
    cut[:, :, 2] = np.einsum("bd,c->bcd", eye, low)
    cut[:, :, 3] = np.einsum("bd,c->bcd", eye, high)
    put = np.zeros((4, SIDE, F, F), np.float32)
    put[0, :, 0, :] = tangent.T
    put[1, :, F - 1, :] = tangent.T
    put[2, :, :, 0] = tangent.T
    put[3, :, :, F - 1] = tangent.T
    columns = np.zeros((3, LANES, LANES), np.float32)
    lines = np.zeros((LANES, 8, LANES), np.float32)
    ghost = np.zeros((LANES, 4, F * F), np.float32)
    for k in range(3):
        columns[k, : SIDE * SIDE, k * WIDE : (k + 1) * WIDE] = cut.reshape(SIDE * SIDE, WIDE)
        ghost[k * WIDE : (k + 1) * WIDE, k] = put.reshape(WIDE, F * F)
        for half in range(2):
            for side in range(2):
                for c in range(SIDE):
                    lane = half * 64 + k * 2 * SIDE + side * SIDE + c
                    window = side * (SIDE - 1) * SIDE + c
                    lines[lane, half] = columns[k, window]
                    lines[lane, 2 + 2 * k + half, window] = 1.0
    ghost[: SIDE * SIDE, 3] = np.einsum("sb,tc->bcst", tangent, tangent).reshape(SIDE * SIDE, F * F)
    mean = np.zeros((F * F, LANES), np.float32)
    for y in range(F):
        for z in range(F):
            for half in range(2):
                mean[y * F + z, half * 64 + (y // 2) * B + z // 2] = 0.125
    bf = jnp.bfloat16
    return (
        jnp.asarray(columns.reshape(3 * LANES, LANES), bf),
        jnp.asarray(lines.reshape(LANES, 8 * LANES), bf),
        jnp.asarray(ghost.reshape(LANES, 4 * F * F), bf),
        jnp.asarray(mean, bf),
    )


def div(a, n):
    return lax.div(a, jnp.full_like(a, n))


def rem(a, n):
    return lax.rem(a, jnp.full_like(a, n))


def split(a):
    high = a.astype(jnp.bfloat16)
    return high, (a - high.astype(jnp.float32)).astype(jnp.bfloat16)


def dot(a, b):
    return jnp.dot(a, b, preferred_element_type=jnp.float32)


def exact_right(a, b):
    high, low = split(a)
    return dot(high, b) + dot(low, b)


def exact_left(a, b):
    a = a.astype(jnp.bfloat16)
    high, low = split(b)
    return dot(a, high) + dot(a, low)


def pick(mask, value):
    return jnp.max(jnp.where(mask, value, -1))


def as_float(cond):
    return jnp.where(cond, 1.0, 0.0).astype(jnp.float32)


def grid_tables(bricks, ny, nz, corners, slot_ref):
    x, y, z = corners[0:1, :], corners[1:2, :], corners[2:3, :]
    slot = slot_ref[...]
    brick = (div(x, bricks[0]) * ny + div(y, bricks[1])) * nz + div(z, bricks[2])
    place = rem(y, bricks[1]) * bricks[2] + rem(z, bricks[2])
    return x, y, slot, brick, place


def step_kernel(
    dims, corners_in, slot_in, near_in, coarse, fine_in, visc_in, columns_in, lines_in, ghost_in, mean_in,
    fine_out, picked,
    corners, slot_ref, near_ref, field, fine, visc, columns, lines, ghost, mean,
    window, z_send_a, z_send_y, z_recv_a, z_recv_y, a_buf, y_buf, p1_buf, p2_send, p2_buf, e_send, e_buf,
    advs, m_send, m_buf, q_send, q_buf,
    local_sem, z_sem, y_send_sem, y_recv_sem, x_send_sem, x_recv_sem,
):
    nx, ny, nz, bx, by, bz = dims
    ix, iy, iz = lax.axis_index("gx"), lax.axis_index("gy"), lax.axis_index("gz")
    me = (ix * ny + iy) * nz + iz
    mesh_id = pl.DeviceIdType.MESH

    def local(i, src, dst):
        return pltpu.make_async_copy(src, dst, local_sem.at[i])

    tiles = bz // LANES
    field_loads = [
        local(6 + t, coarse.at[:, t * LANES : (t + 1) * LANES], field.at[t]) for t in range(tiles)
    ]
    loads = [
        local(0, fine_in, fine), local(1, columns_in, columns), local(2, visc_in, visc),
        local(3, lines_in, lines), local(4, ghost_in, ghost), local(5, mean_in, mean),
    ]
    fine_load, columns_load, visc_load, lines_load, ghost_load, mean_load = loads
    first = 6 + tiles
    table_loads = [
        local(first, corners_in, corners), local(first + 1, slot_in, slot_ref), local(first + 2, near_in, near_ref)
    ]
    for load in table_loads + [fine_load] + field_loads + loads[1:]:
        load.start()

    def y_peer(o):
        return lax.rem(iy + o, ny)

    def x_peer(o):
        return lax.rem(ix + o, nx)

    barrier = pltpu.get_barrier_semaphore()
    pl.semaphore_signal(barrier, inc=1, device_id={"gz": 1 - iz}, device_id_type=mesh_id)

    def greet_y(o, c):
        pl.semaphore_signal(barrier, inc=1, device_id={"gy": y_peer(o)}, device_id_type=mesh_id)
        return c

    def greet_x(o, c):
        pl.semaphore_signal(barrier, inc=1, device_id={"gx": x_peer(o)}, device_id_type=mesh_id)
        return c

    lax.fori_loop(1, ny, greet_y, 0)
    lax.fori_loop(1, nx, greet_x, 0)

    def y_copy(which, o, src, dst):
        return pltpu.make_async_remote_copy(
            src_ref=src, dst_ref=dst, send_sem=y_send_sem.at[which, o], recv_sem=y_recv_sem.at[which, o],
            device_id={"gy": y_peer(o)}, device_id_type=mesh_id,
        )

    def x_copy(which, o, src, dst):
        return pltpu.make_async_remote_copy(
            src_ref=src, dst_ref=dst, send_sem=x_send_sem.at[which, o], recv_sem=x_recv_sem.at[which, o],
            device_id={"gx": x_peer(o)}, device_id_type=mesh_id,
        )

    def z_copy(which, src, dst):
        return pltpu.make_async_remote_copy(
            src_ref=src, dst_ref=dst, send_sem=z_sem.at[0, which], recv_sem=z_sem.at[1, which],
            device_id={"gz": 1 - iz}, device_id_type=mesh_id,
        )

    def run(count, make, action):
        def body(o, c):
            getattr(make(o), action)()
            return c

        lax.fori_loop(1, count, body, 0)

    for load in table_loads:
        load.wait()
    gx_, gy_, slot, brick, place = grid_tables((bx, by, bz), ny, nz, corners, slot_ref)
    home = div(gx_, bx) * ny + div(gy_, by)
    box = div(rem(gx_, bx), B)
    dev = div(slot, SLOTS)
    count = slot.shape[1]
    g_row = lax.broadcasted_iota(jnp.int32, (count, count), 0)
    g_col = lax.broadcasted_iota(jnp.int32, (count, count), 1)
    slot_col = jnp.max(jnp.where(g_row == g_col, slot, -1), axis=1, keepdims=True)
    near_slot = []
    far_dev = []
    for side in range(2):
        m = jnp.max(jnp.where(g_row == near_ref[side : side + 1, :], slot_col, -1), axis=0, keepdims=True)
        near_slot.append(m)
        d = div(jnp.maximum(m, 0), SLOTS)
        far_dev.append(jnp.where((m >= 0) & (d != dev), d, -1))

    def anchor(ox, oy, gz):
        hx, hy = ix + ox, iy + oy
        inside = (hx >= 0) & (hx < nx) & (hy >= 0) & (hy < ny)
        code = jnp.maximum(pick(brick == jnp.where(inside, (hx * ny + hy) * nz + gz, -5), place), 0)
        return lax.div(code, bz), lax.rem(code, bz)

    mine = dev == me
    own_slot = [pick(mine & (box == j), rem(slot, SLOTS)) for j in range(SLOTS)]

    fine_load.wait()
    for i in range(IFACES):
        for k in range(3):
            if i == 0:
                row = fine[k, jnp.maximum(own_slot[0], 0), 0:1]
            elif i == SLOTS:
                row = fine[k, jnp.maximum(own_slot[SLOTS - 1], 0), F - 1 : F]
            else:
                below = fine[k, jnp.maximum(own_slot[i - 1], 0), F - 1 : F]
                above = fine[k, jnp.maximum(own_slot[i], 0), 0:1]
                row = jnp.where(own_slot[i - 1] >= 0, below, above)
            p1_buf[iy, i * 3 + k : i * 3 + k + 1] = row
    p1_buf[iy, PLANE_ROWS - 1 : PLANE_ROWS] = jnp.zeros((1, F * F), jnp.float32)
    pl.semaphore_wait(barrier, nx + ny - 1)

    def p1_copy(o):
        return y_copy(0, o, p1_buf.at[iy], p1_buf.at[iy])

    run(ny, p1_copy, "start")

    stride = bx * by
    lane1 = lax.broadcasted_iota(jnp.int32, (1, LANES), 1)
    lane_b = div(lane1, SIDE)
    lane_c = rem(lane1, SIDE)
    half_lane = rem(lane1, 64)
    half_c = rem(half_lane, SIDE)
    line_id = div(half_lane, SIDE)

    def lines_at(z, start, size, step):
        z = lax.rem(z - 1 + bz, bz)
        tile, low = lax.div(z, LANES), lax.rem(z, LANES)
        after = lax.rem(tile + 1, tiles)

        def get(t):
            return field[t, pl.ds(start, size, step)] if step > 1 else field[t, pl.ds(start, size)]

        lane = lax.broadcasted_iota(jnp.int32, (size, LANES), 1)
        return jnp.where(lane >= low, get(tile), get(after)), low

    def shifted(z, start, size, step, to):
        value, low = lines_at(z, start, size, step)
        return pltpu.roll(value, lax.rem(to - low + LANES, LANES), 1)

    def z_weight(z, ids, same):
        first, last = z == 0, z == bz - B
        if same:
            return jnp.where(ids == 0, as_float(~first), jnp.where(ids == SIDE - 1, as_float(~last), 1.0))
        first = as_float(first & (iz == 0))
        last = as_float(last & (iz == 1))
        return jnp.where(ids == 0, first, jnp.where(ids == SIDE - 1, last, 0.0))

    def pack(gz, same, a_to, y_to):
        y, z = anchor(0, 0, gz)
        weight = z_weight(z, lane_c, same)
        weight = weight * jnp.where(lane_b == 0, as_float(y > 0), jnp.where(lane_b == SIDE - 1, as_float(y < by - B), 1.0))
        weight = jnp.where(lane1 < SIDE * SIDE, weight, 0.0)
        for k in range(3):
            acc = jnp.zeros((bx, LANES), jnp.float32)
            for b in range(SIDE):
                row = jnp.clip(y - 1 + b, 0, by - 1)
                acc = jnp.where(lane_b == b, shifted(z, k * stride + row, bx, by, SIDE * b), acc)
            window[k, 0:bx] = acc * weight
        for n, ox in enumerate((1, -1)):
            y, z = anchor(ox, 0, gz)
            weight = z_weight(z, lane_c, same)
            weight = weight * jnp.where(
                lane_b == 0, as_float(y > 0), jnp.where(lane_b == SIDE - 1, as_float(y < by - B), 1.0)
            )
            weight = jnp.where(lane1 < SIDE * SIDE, weight, 0.0)
            x = bx - 1 if ox > 0 else 0
            for k in range(3):
                acc = jnp.zeros((1, LANES), jnp.float32)
                for b in range(SIDE):
                    row = jnp.clip(y - 1 + b, 0, by - 1)
                    acc = jnp.where(lane_b == b, shifted(z, k * stride + x * by + row, 1, 1, SIDE * b), acc)
                window[k, bx + n : bx + n + 1] = acc * weight
        total = jnp.zeros((E_ROWS, LANES), jnp.float32)
        for k in range(3):
            total += exact_right(window[k], columns[k * LANES : (k + 1) * LANES])
            for side in range(2):
                at = bx + 2 + 2 * k + side
                inner = 0 if side == 0 else bx - 1
                a_to[at : at + 1] = window[k, inner : inner + 1]
                a_to[at + 6 : at + 7] = window[k, bx + side : bx + side + 1]
        a_to[0 : bx + 2] = total[0 : bx + 2]
        half = bx // 2
        main = jnp.zeros((half, LANES), jnp.float32)
        ends = [jnp.zeros((1, LANES), jnp.float32) for _ in range(2)]
        for side, oy in enumerate((1, -1)):
            row = by - 1 if oy > 0 else 0
            edge = 0 if oy > 0 else by - B
            y, z = anchor(0, oy, gz)
            weight = z_weight(z, half_c, same) * as_float(y == edge)
            for k in range(3):
                to = k * 2 * SIDE + side * SIDE
                for h in range(2):
                    value = shifted(z, k * stride + h * half * by + row, half, by, to + 64 * h)
                    main = jnp.where((line_id == 2 * k + side) & (div(lane1, 64) == h), value * weight, main)
            for n, ox in enumerate((1, -1)):
                y, z = anchor(ox, oy, gz)
                weight = z_weight(z, half_c, same) * as_float(y == edge)
                x = bx - 1 if ox > 0 else 0
                for k in range(3):
                    to = k * 2 * SIDE + side * SIDE
                    value = shifted(z, k * stride + x * by + row, 1, 1, to)
                    ends[n] = jnp.where((line_id == 2 * k + side) & (lane1 < 64), value * weight, ends[n])
        y_to[0:half] = main
        y_to[half : half + 1] = ends[0]
        y_to[half + 1 : half + 2] = ends[1]

    a_own, y_own = a_buf.at[iy], y_buf.at[iy]
    for k in range(3):
        window[k, bx + 2 : E_ROWS] = jnp.zeros((E_ROWS - bx - 2, LANES), jnp.float32)
    for buf in (z_send_a, a_own):
        buf[bx + 14 : A_ROWS] = jnp.zeros((A_ROWS - bx - 14, LANES), jnp.float32)
    for buf in (z_send_y, y_own):
        buf[bx // 2 + 2 : Y_ROWS] = jnp.zeros((Y_ROWS - bx // 2 - 2, LANES), jnp.float32)
    for load in field_loads:
        load.wait()
    columns_load.wait()
    pack(1 - iz, False, z_send_a, z_send_y)
    to_partner = [z_copy(0, z_send_a, z_recv_a), z_copy(1, z_send_y, z_recv_y)]
    for c in to_partner:
        c.start()
    pack(iz, True, a_own, y_own)
    for c in to_partner:
        c.wait()
    a_own[...] += z_recv_a[...]
    y_own[...] += z_recv_y[...]

    def a_copy(o):
        return y_copy(1, o, a_own, a_own)

    def l_copy(o):
        return y_copy(2, o, y_own, y_own)

    run(ny, a_copy, "start")
    run(ny, l_copy, "start")

    run(ny, p1_copy, "wait")
    for t in range(nx):
        target = (t * ny + iy) * nz + iz
        there = dev == target
        for i in range(IFACES):
            low_need = there & (box == i)
            high_need = there & (box == i - 1)
            code = jnp.where(low_need, far_dev[0], jnp.where(high_need, far_dev[1], -1))
            source = jnp.maximum(jnp.max(code), 0)
            sy = lax.rem(lax.div(source, nz), ny)
            at = SLOTS if i == 0 else (0 if i == SLOTS else i)
            p2_send[t, 3 * i : 3 * i + 3] = p1_buf[sy, 3 * at : 3 * at + 3]
        p2_send[t, PLANE_ROWS - 1 : PLANE_ROWS] = jnp.zeros((1, F * F), jnp.float32)
    p2_buf[ix] = p2_send[ix]

    def p2_copy(o):
        return x_copy(0, o, p2_send.at[x_peer(o)], p2_buf.at[ix])

    run(nx, p2_copy, "start")

    visc_load.wait()
    slots = []
    for s in range(SLOTS):
        here = slot == me * SLOTS + s
        b = pick(here, box)
        near = []
        for side in range(2):
            m = pick(here, near_slot[side])
            n = jnp.maximum(m, 0)
            d = lax.div(n, SLOTS)
            near.append((m >= 0, d == me, lax.rem(n, SLOTS), lax.div(d, ny * nz)))
        slots.append((b >= 0, jnp.maximum(b, 0), near))
    homes = [pick(dev == (t * ny + iy) * nz + iz, home) for t in range(nx)]
    holders = [
        [jnp.maximum(pick((brick == (ix * ny + t) * nz + iz) & (box == j), slot), 0) for j in range(SLOTS)]
        for t in range(ny)
    ]

    lane = lax.broadcasted_iota(jnp.int32, (F, F * F), 1)
    row = lax.broadcasted_iota(jnp.int32, (F, F * F), 0)
    lz = lane % F

    def bulk(s, c):
        cv = step_rate * visc[s]
        for k in range(3):
            v = fine[k, s]
            total = jnp.where(row == 0, 0.0, pltpu.roll(v, 1, 0))
            total += jnp.where(row == F - 1, 0.0, pltpu.roll(v, F - 1, 0))
            total += jnp.where(lane < F, 0.0, pltpu.roll(v, F, 1))
            total += jnp.where(lane >= F * F - F, 0.0, pltpu.roll(v, F * F - F, 1))
            total += jnp.where(lz == 0, 0.0, pltpu.roll(v, 1, 1))
            total += jnp.where(lz == F - 1, 0.0, pltpu.roll(v, F * F - 1, 1))
            at = pl.multiple_of((s * 3 + k) * F, F)
            value = v + cv * (total - 6.0 * v)
            advs[0, pl.ds(at, F)] = value[:, :LANES]
            advs[1, pl.ds(at, F)] = value[:, LANES:]
        return c

    lax.fori_loop(0, SLOTS, bulk, 0)

    run(ny, a_copy, "wait")
    run(ny, l_copy, "wait")
    lines_load.wait()
    half = bx // 2
    low_line = rem(line_id, 2) == 0
    for t in range(nx):
        code = jnp.maximum(homes[t], 0)
        hx, hy = lax.div(code, ny), lax.rem(code, ny)
        d = hx - ix
        same, up_one, down_one = as_float(d == 0), as_float(d == 1), as_float(d == -1)
        lower = y_buf[jnp.maximum(hy - 1, 0)] * as_float(hy > 0)
        upper = y_buf[jnp.minimum(hy + 1, ny - 1)] * as_float(hy < ny - 1)
        extra = exact_right(jnp.where(low_line, lower, upper), lines[...])
        own = a_buf[hy]
        e_send[t, 0:half] = (own[0:half] + extra[0:half, 0:LANES]) * same
        e_send[t, half:bx] = (own[half:bx] + extra[0:half, LANES : 2 * LANES]) * same
        e_send[t, bx : bx + 1] = (own[bx : bx + 1] + extra[half : half + 1, 0:LANES]) * up_one
        e_send[t, bx + 1 : bx + 2] = (own[bx + 1 : bx + 2] + extra[half + 1 : half + 2, 0:LANES]) * down_one
        for k in range(3):
            for side in range(2):
                at = bx + 2 + 2 * k + side
                first = (2 + 2 * k + side) * LANES
                from_row = 0 if side == 0 else half - 1
                inner = own[at : at + 1] + extra[from_row : from_row + 1, first : first + LANES]
                first = (2 + 2 * k) * LANES
                outer = own[at + 6 : at + 7] + extra[half + side : half + side + 1, first : first + LANES]
                e_send[t, at : at + 1] = inner * (0.25 * same) + outer * (0.75 * (down_one if side else up_one))
    e_buf[ix] = e_send[ix]

    def e_copy(o):
        return x_copy(1, o, e_send.at[x_peer(o)], e_buf.at[ix])

    run(nx, e_copy, "start")

    shape = (SLOTS * F, E_ROWS)
    out_line = lax.broadcasted_iota(jnp.int32, shape, 0)
    from_line = lax.broadcasted_iota(jnp.int32, shape, 1)
    boxes = jnp.full(shape, slots[0][1], jnp.int32)
    for s in range(1, SLOTS):
        boxes = jnp.where(out_line // F == s, slots[s][1], boxes)
    f_id = out_line % F
    center = B * boxes + f_id // 2
    other = jnp.where(f_id % 2 == 0, center - 1, center + 1)
    other = jnp.where(other < 0, bx, jnp.where(other >= bx, bx + 1, other))
    blend = jnp.where(from_line == center, 0.75, jnp.where(from_line == other, 0.25, 0.0))
    run(nx, p2_copy, "wait")
    ghost_load.wait()
    run(nx, e_copy, "wait")
    total = e_buf[0]
    for t in range(1, nx):
        total += e_buf[t]
    along = exact_left(blend, total)
    ghosts = exact_right(along, ghost[:, 0 : 3 * F * F])
    faces = exact_right(total[bx : E_ROWS], ghost[:, 3 * F * F :])
    mean_load.wait()
    for s in range(SLOTS):
        active, b, near = slots[s]
        cv = step_rate * visc[s]
        for k in range(3):
            ends = []
            for side in range(2):
                has, is_local, n, sx = near[side]
                x = (F - 1) * (1 - side)
                far = p2_buf[sx, pl.ds(3 * (b + side) + k, 1)]
                here = fine[k, n][x : x + 1]
                outer = faces[2 + 2 * k + side : 3 + 2 * k + side]
                ends.append(jnp.where(has, jnp.where(is_local, here, far), outer))
            edge = jnp.where(row == 0, ends[0], jnp.where(row == F - 1, ends[1], 0.0))
            at = (s * 3 + k) * F
            ghost_k = ghosts[s * F : s * F + F, k * F * F : (k + 1) * F * F]
            adv = jnp.concatenate([advs[0, at : at + F], advs[1, at : at + F]], axis=1) + cv * (ghost_k + edge)
            advs[0, at : at + F] = adv[:, :LANES]
            advs[1, at : at + F] = adv[:, LANES:]
            fine_out[k, s] = jnp.where(active, adv, 0.0)
    rows = 3 * SLOTS * F // 2
    pairs = [advs[h, pl.ds(0, rows, 2)] + advs[h, pl.ds(1, rows, 2)] for h in range(2)]
    z = exact_right(jnp.concatenate(pairs, axis=1), mean[...])
    lane_m = lax.broadcasted_iota(jnp.int32, (B // 2, LANES), 1)
    for s in range(SLOTS):
        for k in range(3):
            at = (s * 3 + k) * B
            value = jnp.where(lane_m < 64, z[at : at + B // 2], z[at + B // 2 : at + B])
            m_send[s, k * (B // 2) : (k + 1) * (B // 2)] = value

    def m_copy(o):
        return x_copy(2, o, m_send, m_buf.at[ix])

    run(nx, m_copy, "start")
    m_buf[ix] = m_send[...]
    run(nx, m_copy, "wait")
    for t in range(ny):
        for j in range(SLOTS):
            n = holders[t][j]
            q_send[t, j] = m_buf[lax.div(n, SLOTS * nz * ny), lax.rem(n, SLOTS)]

    def q_copy(o):
        return y_copy(3, o, q_send.at[y_peer(o)], q_buf.at[iy])

    run(ny, q_copy, "start")
    q_buf[iy] = q_send[iy]
    owners = [
        jnp.maximum(pick((brick == me) & (box == j), slot), 0) for j in range(SLOTS)
    ]
    run(ny, q_copy, "wait")
    for j in range(SLOTS):
        picked[j] = q_buf[lax.rem(lax.div(owners[j], SLOTS * nz), ny), j]


def final_kernel(dims, corners, slot_ref, field, picked, fine, coarse_out, fine_out, group, sems):
    nx, ny, nz, bx, by, bz = dims
    ix, iy, iz = lax.axis_index("gx"), lax.axis_index("gy"), lax.axis_index("gz")
    me = (ix * ny + iy) * nz + iz
    _, _, _, brick, place = grid_tables((bx, by, bz), ny, nz, corners, slot_ref)
    code = pick(brick == me, place)
    present = code >= 0
    code = jnp.maximum(code, 0)
    y_group = lax.div(lax.div(code, bz), B)
    z = lax.rem(code, bz)
    fine_copy = pltpu.make_async_copy(fine, fine_out, sems.at[0])
    fine_copy.start()

    def plain(g):
        return pltpu.make_async_copy(
            field.at[:, pl.ds(g * B, B)], coarse_out.at[:, pl.ds(g * B, B)], sems.at[1 + g]
        )

    def patched(g):
        return pltpu.make_async_copy(group, coarse_out.at[:, pl.ds(g * B, B)], sems.at[1 + g])

    for g in range(by // B):

        @pl.when(y_group != g)
        def _():
            plain(g).start()

    start = pl.multiple_of(y_group * B, B)
    low = lax.rem(z, LANES)
    tile = lax.div(z, LANES)
    lane = lax.broadcasted_iota(jnp.int32, (B, LANES), 1)
    eight = lane // B
    line = lax.broadcasted_iota(jnp.int32, (B, LANES), 0)
    chosen = eight % B == line
    first_half = (eight - line + 16) % 16 < B
    inside = [(lane >= low) & (lane < low + B) & (tile == t) & present for t in range(bz // LANES)]
    for j in range(SLOTS):
        for at in range(MEAN_ROWS):
            value = jnp.where(chosen, jnp.broadcast_to(picked[j, at : at + 1], (B, LANES)), 0.0)
            for step in (B, 2 * B, 4 * B):
                value += pltpu.roll(value, step, 1)
            swapped = pltpu.roll(value, 64, 1)
            k, a = at // (B // 2), at % (B // 2)
            for h in range(2):
                new = jnp.where(first_half, value, swapped) if h == 0 else jnp.where(first_half, swapped, value)
                x = k * bx + j * B + h * (B // 2) + a
                for t in range(bz // LANES):
                    old = field[x, pl.ds(start, B), t * LANES : (t + 1) * LANES]
                    group[x, :, t * LANES : (t + 1) * LANES] = jnp.where(inside[t], new, old)
    patched(y_group).start()
    for g in range(by // B):
        patched(g).wait()
    fine_copy.wait()


def on_device(coarse_field, fine_field, viscosity, corners, grid_slot, neighbors):
    nx, ny, nz = (lax.axis_size(n) for n in ("gx", "gy", "gz"))
    assert nz == 2
    bx, by, bz = coarse_field.shape[1:]
    dims = (nx, ny, nz, bx, by, bz)
    consts = matrices()
    vmem = pl.BlockSpec(memory_space=pltpu.VMEM)
    hbm = pl.BlockSpec(memory_space=pltpu.HBM)
    stay = functools.partial(pltpu.with_memory_space_constraint, memory_space=pltpu.HBM)
    grids = grid_slot.shape[0]
    f32 = jnp.float32
    dma = pltpu.SemaphoreType.DMA
    tables_in = (corners.T, grid_slot.reshape(1, -1))
    fine_new, picked = pl.pallas_call(
        functools.partial(step_kernel, dims),
        out_shape=(
            jax.ShapeDtypeStruct(fine_field.shape, f32),
            jax.ShapeDtypeStruct((SLOTS, MEAN_ROWS, LANES), f32),
        ),
        in_specs=[hbm] * 10,
        out_specs=(vmem, vmem),
        scratch_shapes=[
            pltpu.VMEM((3, grids), jnp.int32),
            pltpu.VMEM((1, grids), jnp.int32),
            pltpu.VMEM((2, grids), jnp.int32),
            pltpu.VMEM((bz // LANES, 3 * bx * by, LANES), f32),
            pltpu.VMEM(fine_field.shape, f32),
            pltpu.VMEM(viscosity.shape, f32),
        ]
        + [pltpu.VMEM(c.shape, c.dtype) for c in consts]
        + [
            pltpu.VMEM((3, E_ROWS, LANES), f32),
            pltpu.VMEM((A_ROWS, LANES), f32),
            pltpu.VMEM((Y_ROWS, LANES), f32),
            pltpu.VMEM((A_ROWS, LANES), f32),
            pltpu.VMEM((Y_ROWS, LANES), f32),
            pltpu.VMEM((ny, A_ROWS, LANES), f32),
            pltpu.VMEM((ny, Y_ROWS, LANES), f32),
            pltpu.VMEM((ny, PLANE_ROWS, F * F), f32),
            pltpu.VMEM((nx, PLANE_ROWS, F * F), f32),
            pltpu.VMEM((nx, PLANE_ROWS, F * F), f32),
            pltpu.VMEM((nx, E_ROWS, LANES), f32),
            pltpu.VMEM((nx, E_ROWS, LANES), f32),
            pltpu.VMEM((2, 3 * SLOTS * F, LANES), f32),
            pltpu.VMEM((SLOTS, MEAN_ROWS, LANES), f32),
            pltpu.VMEM((nx, SLOTS, MEAN_ROWS, LANES), f32),
            pltpu.VMEM((ny, SLOTS, MEAN_ROWS, LANES), f32),
            pltpu.VMEM((ny, SLOTS, MEAN_ROWS, LANES), f32),
            dma((9 + bz // LANES,)),
            dma((2, 2)),
            dma((4, ny)),
            dma((4, ny)),
            dma((3, nx)),
            dma((3, nx)),
        ],
        compiler_params=pltpu.CompilerParams(collective_id=0, has_side_effects=True, vmem_limit_bytes=24 * MIB),
        name="step",
    )(
        *map(
            stay, (*tables_in, neighbors.T, coarse_field.reshape(3 * bx * by, bz), fine_field, viscosity, *consts)
        )
    )
    coarse_out, fine_out = pl.pallas_call(
        functools.partial(final_kernel, dims),
        out_shape=(
            jax.ShapeDtypeStruct((3 * bx, by, bz), f32),
            jax.ShapeDtypeStruct(fine_field.shape, f32),
        ),
        in_specs=[vmem] * 5,
        out_specs=(hbm, hbm),
        scratch_shapes=[pltpu.VMEM((3 * bx, B, bz), f32), dma((1 + by // B,))],
        compiler_params=pltpu.CompilerParams(vmem_limit_bytes=16 * MIB),
        name="final",
    )(*tables_in, coarse_field.reshape(3 * bx, by, bz), picked, fine_new)
    return fine_out, coarse_out.reshape(coarse_field.shape)


def solution(mesh):
    in_specs = (
        P(None, "gx", "gy", "gz"),
        P(None, ("gx", "gy", "gz"), None, None),
        P(("gx", "gy", "gz"), None, None),
        P(),
        P(),
        P(),
    )
    out_specs = (P(None, ("gx", "gy", "gz"), None, None), P(None, "gx", "gy", "gz"))
    return jax.shard_map(
        on_device, mesh=mesh, in_specs=in_specs, out_specs=out_specs, check_vma=False
    )
```

time: 88.3 us -> 29.1 us (0.33); the launches traced: 87.2 us -> 28.9 us
  Pallas kernels: 43.9 us -> 28.2 us
  local copies, waits for them, and re-layouts: 14.9 us -> 0.01 us
  starting transfers between devices: 12.2 us -> 0 us
  waiting for transfers between devices: 7.26 us -> 0 us
  between operations: 7.38 us -> 0.69 us
  other arithmetic: 1.52 us -> 0 us
    pallas_call x4 -> x2, Pallas kernels: 43.9 us -> 28.2 us  [the longest x1 26.3 us: on_device(): pl.pallas_call(functools.partial(step_kernel, dims), out_shape=(jax.Shape...]
    ppermute x5 -> x0, starting transfers between devices: 12.2 us -> none  [the longest x2 9.05 us: shift(): low = lax.ppermute(high_part, axis, [(i, i + 1) for i in range(count - 1)])]
    ppermute x5 -> x0, waiting for transfers between devices: 7.26 us -> none  [the longest x2 5.61 us: shift(): high = lax.ppermute(low_part, axis, [(i + 1, i) for i in range(count - 1)])]
    dynamic_slice x10 -> x0, local copies, waits for them, and re-layouts: 5.26 us -> none  [cut(): return lax.dynamic_slice_in_dim(a, start, size, axis=2)]
    slice x8 -> x0, local copies, waits for them, and re-layouts: 5.15 us -> none  [the longest x1 2.46 us: cut_slab(): field[..., -1:]]
    unnamed x9 -> x6, local copies, waits for them, and re-layouts: 1.98 us -> 0.01 us
    concatenate x6 -> x0, other arithmetic: 1.17 us -> none  [the longest x3 0.75 us: line(): jnp.concatenate([cut(xlo), wide(cut(field), cut(zlo), cut(zhi)), cut(xhi)...]
  transfers between devices with their start and end apart: 5 -> 0, of which waited for: 4 -> 0; matrix products, arithmetic and copies ran while one was open for 10% -> 0% of each run, Pallas kernels for 5% -> 0%
where the time goes in v1:
time: 29.1 us; the launch traced here: 28.9 us
  Pallas kernels  28.2 us (97%)
  between operations  0.69 us (2%)
    pallas_call x1, Pallas kernels, on_device(): pl.pallas_call(functools.partial(step_kernel, dims), out_shape=(jax.Shape...  26.3 us
    pallas_call x1, Pallas kernels, on_device(): pl.pallas_call(functools.partial(final_kernel, dims), out_shape=(jax.Shap...  1.98 us

profile of v1, /device:TPU:0, one launch (start us, length us, event | category | flops | bytes accessed | tf_op | source)
XLA Modules:
  0.0 28.9 jit_solution(11383047721213455378)
XLA Ops:
  0.6 0.0 copy-start
  0.6 0.0 copy-start.2
  0.7 0.0 copy-start.1
  0.7 26.3 %step.1 = (f32[3,4,16,256]{3,2,1,0:T(8,128)S(1)}, f32[4,12,128]{2,1,0:T(8,128)S(1)}) custom-call(s32[3,64]{1,0:T(4,128)} %bitcast.8, s32[1,64]{1,0:T(1,128)} %bitcast.10, s32[2,64]{1,0:T(2,128)} %bitcast.12, f32[3072,256]{1,0:T(8,128)} %bitcast.6, f32[3,4,16,256]{3,2,1,0:T(8,128)} %fine_in.1, f32[4,16,256]{2,1,0:T(8,128)} %visc_in.1, ...), custom_call_target="tpu_custom_call" | custom-call | tf_op jit(solution)/shard_map/step/pallas_call | solution.py:601
  26.9 0.0 copy-done
  26.9 0.0 copy-done.2
  26.9 0.0 copy-done.1
  27.0 2.0 %final.1 = (f32[96,32,256]{2,1,0:T(8,128)}, f32[3,4,16,256]{3,2,1,0:T(8,128)}) custom-call(s32[3,64]{1,0:T(4,128)S(1)} %bitcast.9, s32[1,64]{1,0:T(1,128)S(1)} %bitcast.11, f32[96,32,256]{2,1,0:T(8,128)S(1)} %bitcast.7, f32[4,12,128]{2,1,0:T(8,128)S(1)} %get-tuple-element.6.picked, f32[3,4,16,256]{3,2,1,0:T(8,128)S(1)} %get-tuple-element.7.fine), custom_call_target="tpu_custom_call" | custom-call | tf_op jit(solution)/shard_map/final/pallas_call | solution.py:650
Async XLA Ops:
  0.6 26.3 %copy-start = (f32[3,32,32,256]{3,2,1,0:T(8,128)S(1)}, f32[3,32,32,256]{3,2,1,0:T(8,128)}, u32[]{:S(2)}) copy-start(f32[3,32,32,256]{3,2,1,0:T(8,128)} %param.10) | copy-start | bytes 9437188
  0.6 26.3 %copy-start.2 = (s32[64]{0:T(128)S(1)}, s32[64]{0:T(128)}, u32[]{:S(2)}) copy-start(s32[64]{0:T(128)} %param.14) | copy-start | bytes 772
  0.7 26.3 %copy-start.1 = (s32[64,3]{0,1:T(4,128)S(1)}, s32[64,3]{0,1:T(4,128)}, u32[]{:S(2)}) copy-start(s32[64,3]{0,1:T(4,128)} %param.13) | copy-start | bytes 2308

commit v2 on v1

v2 whole, which is shorter than its diff:
```python
import functools
import numpy as np
import jax
import jax.numpy as jnp
from jax import lax
from jax.experimental import pallas as pl
from jax.experimental.pallas import tpu as pltpu
from jax.sharding import PartitionSpec as P

B = 8
F = 16
SLOTS = 4
SIDE = B + 2
LANES = 128
WIDE = 4 * SIDE
IFACES = SLOTS + 1
PLANE_LINES = 4
E_ROWS = 48
MEAN_ROWS = 12
step_rate = 0.15
MIB = 1 << 20


def tables():
    tangent = np.zeros((F, SIDE), np.float32)
    for f in range(F):
        c = f // 2 + 1
        tangent[f, c] = 0.75
        tangent[f, c - 1 if f % 2 == 0 else c + 1] = 0.25
    low = np.zeros((SIDE,), np.float32)
    low[0], low[1] = 0.75, 0.25
    return tangent, low, low[::-1].copy()


def matrices():
    tangent, low, high = tables()
    eye = np.eye(SIDE, dtype=np.float32)
    cut = np.zeros((SIDE, SIDE, 4, SIDE), np.float32)
    cut[:, :, 0] = np.einsum("b,cd->bcd", low, eye)
    cut[:, :, 1] = np.einsum("b,cd->bcd", high, eye)
    cut[:, :, 2] = np.einsum("bd,c->bcd", eye, low)
    cut[:, :, 3] = np.einsum("bd,c->bcd", eye, high)
    put = np.zeros((4, SIDE, F, F), np.float32)
    put[0, :, 0, :] = tangent.T
    put[1, :, F - 1, :] = tangent.T
    put[2, :, :, 0] = tangent.T
    put[3, :, :, F - 1] = tangent.T
    columns = np.zeros((3, LANES, LANES), np.float32)
    lines = np.zeros((LANES, 8, LANES), np.float32)
    ghost = np.zeros((LANES, 4, F * F), np.float32)
    for k in range(3):
        columns[k, : SIDE * SIDE, k * WIDE : (k + 1) * WIDE] = cut.reshape(SIDE * SIDE, WIDE)
        ghost[k * WIDE : (k + 1) * WIDE, k] = put.reshape(WIDE, F * F)
        for half in range(2):
            for side in range(2):
                for c in range(SIDE):
                    lane = half * 64 + k * 2 * SIDE + side * SIDE + c
                    window = side * (SIDE - 1) * SIDE + c
                    lines[lane, half] = columns[k, window]
                    lines[lane, 2 + 2 * k + half, window] = 1.0
    ghost[: SIDE * SIDE, 3] = np.einsum("sb,tc->bcst", tangent, tangent).reshape(SIDE * SIDE, F * F)
    mean = np.zeros((F * F, LANES), np.float32)
    for y in range(F):
        for z in range(F):
            for half in range(2):
                mean[y * F + z, half * 64 + (y // 2) * B + z // 2] = 0.125
    rim = [y * F + z for y in range(F) for z in range(F) if y in (0, F - 1) or z in (0, F - 1)]
    take = np.zeros((F * F, LANES), np.float32)
    rim_ghost = np.zeros((LANES, 3, LANES), np.float32)
    rim_mean = np.zeros((LANES, LANES), np.float32)
    for m, at in enumerate(rim):
        for half in range(2):
            take[at, half * 64 + m] = 1.0
            rim_ghost[:, :, half * 64 + m] = ghost[:, :3, at]
            rim_mean[half * 64 + m, half * 64 + (at // F // 2) * B + at % F // 2] = 0.125
    shapes = (
        columns.reshape(3 * LANES, LANES), lines.reshape(LANES, 8 * LANES), ghost.reshape(LANES, 4 * F * F),
        mean, take, rim_ghost.reshape(LANES, 3 * LANES), rim_mean,
    )
    return tuple(jnp.asarray(a, jnp.bfloat16) for a in shapes)


def div(a, n):
    return lax.div(a, jnp.full_like(a, n))


def rem(a, n):
    return lax.rem(a, jnp.full_like(a, n))


def split(a):
    high = a.astype(jnp.bfloat16)
    return high, (a - high.astype(jnp.float32)).astype(jnp.bfloat16)


def dot(a, b):
    return jnp.dot(a, b, preferred_element_type=jnp.float32)


def exact_right(a, b):
    high, low = split(a)
    return dot(high, b) + dot(low, b)


def exact_left(a, b):
    a = a.astype(jnp.bfloat16)
    high, low = split(b)
    return dot(a, high) + dot(a, low)


def pick(mask, value):
    return jnp.max(jnp.where(mask, value, -1))


def as_float(cond):
    return jnp.where(cond, 1.0, 0.0).astype(jnp.float32)


def grid_tables(bricks, ny, nz, corners, slot_ref):
    x, y, z = corners[0:1, :], corners[1:2, :], corners[2:3, :]
    slot = slot_ref[...]
    brick = (div(x, bricks[0]) * ny + div(y, bricks[1])) * nz + div(z, bricks[2])
    place = rem(y, bricks[1]) * bricks[2] + rem(z, bricks[2])
    return x, y, slot, brick, place


def step_kernel(
    dims, corners_in, slot_in, near_in, coarse, fine_in, visc_in,
    columns_in, lines_in, ghost_in, mean_in, take_in, rim_ghost_in, rim_mean_in,
    fine_out, picked,
    corners, slot_ref, near_ref, field, fine, visc, columns, lines, ghost, mean, take, rim_ghost, rim_mean,
    window, z_send, z_recv, w_buf, p_buf, f_buf, p2_send, p2_buf, e_send, e_buf,
    advs, m_send, m_buf, c_send, c_buf, qm_send, qm_buf, qc_send, qc_buf, qf_send, qf_buf,
    local_sem, z_sem, y_send_sem, y_recv_sem, x_send_sem, x_recv_sem,
):
    nx, ny, nz, bx, by, bz = dims
    ix, iy, iz = lax.axis_index("gx"), lax.axis_index("gy"), lax.axis_index("gz")
    me = (ix * ny + iy) * nz + iz
    mesh_id = pl.DeviceIdType.MESH
    tiles = bz // LANES
    half = bx // 2
    pitch = by + 8

    pairs = [
        (corners_in, corners), (slot_in, slot_ref), (near_in, near_ref), (fine_in, fine), (visc_in, visc),
    ]
    for t in range(tiles):
        pairs.append((coarse.at[:, :, t * LANES : (t + 1) * LANES], field.at[t, :, 0:by]))
    pairs += [
        (mean_in, mean), (take_in, take), (columns_in, columns), (lines_in, lines), (ghost_in, ghost),
        (rim_ghost_in, rim_ghost), (rim_mean_in, rim_mean),
    ]
    loads = [pltpu.make_async_copy(src, dst, local_sem.at[i]) for i, (src, dst) in enumerate(pairs)]
    for load in loads:
        load.start()
    table_loads, fine_load, visc_load, field_loads = loads[:3], loads[3], loads[4], loads[5 : 5 + tiles]
    mean_load, take_load, columns_load, lines_load, ghost_load, rim_ghost_load, rim_mean_load = loads[5 + tiles :]

    def y_peer(o):
        return lax.rem(iy + o, ny)

    def x_peer(o):
        return lax.rem(ix + o, nx)

    barrier = pltpu.get_barrier_semaphore()
    pl.semaphore_signal(barrier, inc=1, device_id={"gz": 1 - iz}, device_id_type=mesh_id)

    def greet_y(o, c):
        pl.semaphore_signal(barrier, inc=1, device_id={"gy": y_peer(o)}, device_id_type=mesh_id)
        return c

    def greet_x(o, c):
        pl.semaphore_signal(barrier, inc=1, device_id={"gx": x_peer(o)}, device_id_type=mesh_id)
        return c

    lax.fori_loop(1, ny, greet_y, 0)
    lax.fori_loop(1, nx, greet_x, 0)

    def y_copy(which, o, src, dst):
        return pltpu.make_async_remote_copy(
            src_ref=src, dst_ref=dst, send_sem=y_send_sem.at[which, o - 1], recv_sem=y_recv_sem.at[which, o - 1],
            device_id={"gy": y_peer(o)}, device_id_type=mesh_id,
        )

    def x_copy(which, o, src, dst):
        return pltpu.make_async_remote_copy(
            src_ref=src, dst_ref=dst, send_sem=x_send_sem.at[which, o - 1], recv_sem=x_recv_sem.at[which, o - 1],
            device_id={"gx": x_peer(o)}, device_id_type=mesh_id,
        )

    def run(count, makes, action):
        def body(o, c):
            for make in makes:
                getattr(make(o), action)()
            return c

        lax.fori_loop(1, count, body, 0)

    for load in table_loads:
        load.wait()
    gx_, gy_, slot, brick, place = grid_tables((bx, by, bz), ny, nz, corners, slot_ref)
    home = div(gx_, bx) * ny + div(gy_, by)
    box = div(rem(gx_, bx), B)
    dev = div(slot, SLOTS)
    count = slot.shape[1]
    g_row = lax.broadcasted_iota(jnp.int32, (count, count), 0)
    g_col = lax.broadcasted_iota(jnp.int32, (count, count), 1)
    slot_col = jnp.max(jnp.where(g_row == g_col, slot, -1), axis=1, keepdims=True)
    near_slot = []
    far_dev = []
    for side in range(2):
        m = jnp.max(jnp.where(g_row == near_ref[side : side + 1, :], slot_col, -1), axis=0, keepdims=True)
        near_slot.append(m)
        d = div(jnp.maximum(m, 0), SLOTS)
        far_dev.append(jnp.where((m >= 0) & (d != dev), d, -1))

    def anchor(ox, oy, gz):
        hx, hy = ix + ox, iy + oy
        inside = (hx >= 0) & (hx < nx) & (hy >= 0) & (hy < ny)
        code = jnp.maximum(pick(brick == jnp.where(inside, (hx * ny + hy) * nz + gz, -5), place), 0)
        return lax.div(code, bz), lax.rem(code, bz)

    mine = dev == me
    own_slot = [pick(mine & (box == j), rem(slot, SLOTS)) for j in range(SLOTS)]
    slots = []
    for s in range(SLOTS):
        here = slot == me * SLOTS + s
        b = pick(here, box)
        near = []
        for side in range(2):
            m = pick(here, near_slot[side])
            n = jnp.maximum(m, 0)
            d = lax.div(n, SLOTS)
            near.append((m >= 0, d == me, lax.rem(n, SLOTS), lax.div(d, ny * nz)))
        slots.append((b >= 0, jnp.maximum(b, 0), near))
    anchors = [
        {(ox, oy): anchor(ox, oy, gz) for ox in (-1, 0, 1) for oy in (-1, 0, 1)} for gz in (1 - iz, iz)
    ]

    fine_load.wait()
    visc_load.wait()
    for i in range(IFACES):
        below = jnp.maximum(own_slot[max(i - 1, 0)], 0)
        above = jnp.maximum(own_slot[min(i, SLOTS - 1)], 0)
        for k in range(PLANE_LINES):
            def line(n, x):
                return fine[k, n, x : x + 1] if k < 3 else step_rate * visc[n, x : x + 1]

            if i == 0:
                value = line(above, 0)
            elif i == SLOTS:
                value = line(below, F - 1)
            else:
                value = jnp.where(own_slot[i - 1] >= 0, line(below, F - 1), line(above, 0))
            p_buf[iy, i, k : k + 1] = value
    pl.semaphore_wait(barrier, nx + ny - 1)
    own_planes = p_buf.at[iy]

    def p1_copy(o):
        return y_copy(0, o, own_planes, own_planes)

    def f_copy(o):
        return x_copy(0, o, own_planes, f_buf.at[ix])

    run(ny, [p1_copy], "start")
    run(nx, [f_copy], "start")
    f_buf[ix] = p_buf[iy]

    lane = lax.broadcasted_iota(jnp.int32, (F, F * F), 1)
    row = lax.broadcasted_iota(jnp.int32, (F, F * F), 0)
    lz = lane % F
    for s in range(SLOTS):
        cv = step_rate * visc[s]
        for k in range(3):
            v = fine[k, s]
            ends = []
            for side in range(2):
                has, is_local, n, _ = slots[s][2][side]
                x = (F - 1) * (1 - side)
                ends.append(fine[k, n][x : x + 1] * as_float(has & is_local))
            total = jnp.where(row == 0, ends[0], pltpu.roll(v, 1, 0))
            total += jnp.where(row == F - 1, ends[1], pltpu.roll(v, F - 1, 0))
            total += jnp.where(lane < F, 0.0, pltpu.roll(v, F, 1))
            total += jnp.where(lane >= F * F - F, 0.0, pltpu.roll(v, F * F - F, 1))
            total += jnp.where(lz == 0, 0.0, pltpu.roll(v, 1, 1))
            total += jnp.where(lz == F - 1, 0.0, pltpu.roll(v, F * F - 1, 1))
            at = (s * 3 + k) * F
            value = v + cv * (total - 6.0 * v)
            advs[0, at : at + F] = value[:, :LANES]
            advs[1, at : at + F] = value[:, LANES:]
    rows = 3 * SLOTS * F // 2
    mean_load.wait()
    sums = [advs[h, pl.ds(0, rows, 2)] + advs[h, pl.ds(1, rows, 2)] for h in range(2)]
    z = exact_right(jnp.concatenate(sums, axis=1), mean[...])
    quarter = B // 2
    lane_m = lax.broadcasted_iota(jnp.int32, (quarter, LANES), 1)
    for s in range(SLOTS):
        for k in range(3):
            at = (s * 3 + k) * B
            m_send[s, k * quarter : (k + 1) * quarter] = jnp.where(
                lane_m < 64, z[at : at + quarter], z[at + quarter : at + B]
            )
    take_load.wait()
    lane_f = lax.broadcasted_iota(jnp.int32, (F, LANES), 1)
    rims = exact_right(step_rate * visc[...].reshape(SLOTS * F, F * F), take[...])
    for s in range(SLOTS // 2):
        low, high = rims[s * F : (s + 1) * F], rims[(s + 2) * F : (s + 3) * F]
        c_send[s] = jnp.where(lane_f < 64, low, high)

    def m_copy(o):
        return x_copy(1, o, m_send, m_buf.at[ix])

    def c_copy(o):
        return x_copy(2, o, c_send, c_buf.at[ix])

    run(nx, [m_copy, c_copy], "start")
    m_buf[ix] = m_send[...]
    c_buf[ix] = c_send[...]

    flat = field.reshape(tiles, 3 * bx * pitch, LANES)
    stride = bx * pitch
    lane1 = lax.broadcasted_iota(jnp.int32, (1, LANES), 1)
    lane_b = div(lane1, SIDE)
    lane_c = rem(lane1, SIDE)
    half_lane = rem(lane1, 64)
    half_c = rem(half_lane, SIDE)
    line_id = div(half_lane, SIDE)

    def shifted(z, same, start, size, step, to):
        def get(t):
            return flat[t, pl.ds(start, size, step)] if size > 1 else flat[t, pl.ds(start, 1)]

        z = lax.rem(z - 1 + bz, bz)
        tile, low = lax.div(z, LANES), lax.rem(z, LANES)
        if same:
            lane = lax.broadcasted_iota(jnp.int32, (size, LANES), 1)
            value = jnp.where(lane >= low, get(tile), get(lax.rem(tile + 1, tiles)))
        else:
            value = get((tiles - 1) * (1 - iz))
        return pltpu.roll(value, lax.rem(to - low + LANES, LANES), 1)

    def z_weight(z, ids, same):
        first, last = z == 0, z == bz - B
        if same:
            return jnp.where(ids == 0, as_float(~first), jnp.where(ids == SIDE - 1, as_float(~last), 1.0))
        first = as_float(first & (iz == 0))
        last = as_float(last & (iz == 1))
        return jnp.where(ids == 0, first, jnp.where(ids == SIDE - 1, last, 0.0))

    def weights(y, z, same):
        weight = z_weight(z, lane_c, same)
        weight = weight * jnp.where(
            lane_b == 0, as_float(y > 0), jnp.where(lane_b == SIDE - 1, as_float(y < by - B), 1.0)
        )
        return jnp.where(lane1 < SIDE * SIDE, weight, 0.0)

    edge_at = bx + half
    line_at = edge_at + 2
    inner_at = line_at + 2
    outer_at = inner_at + 6

    def pack(place, same, to_ref):
        y, z = place[0, 0]
        weight = weights(y, z, same)
        for k in range(3):
            acc = jnp.zeros((bx, LANES), jnp.float32)
            for b in range(SIDE):
                at = jnp.clip(y - 1 + b, 0, by - 1)
                value = shifted(z, same, k * stride + at, bx, pitch, SIDE * b)
                acc = jnp.where(lane_b == b, value, acc)
            window[k, 0:bx] = acc * weight
        for n, ox in enumerate((1, -1)):
            y, z = place[ox, 0]
            weight = weights(y, z, same)
            x = bx - 1 if ox > 0 else 0
            acc = jnp.zeros((3, LANES), jnp.float32)
            for b in range(SIDE):
                at = jnp.clip(y - 1 + b, 0, by - 1)
                acc = jnp.where(lane_b == b, shifted(z, same, x * pitch + at, 3, stride, SIDE * b), acc)
            acc = acc * weight
            for k in range(3):
                window[k, bx + n : bx + n + 1] = acc[k : k + 1]
        total = jnp.zeros((bx + 8, LANES), jnp.float32)
        for k in range(3):
            total += exact_right(window[k], columns[k * LANES : (k + 1) * LANES])
            for side in range(2):
                at = inner_at + 2 * k + side
                inner = 0 if side == 0 else bx - 1
                to_ref[at : at + 1] = window[k, inner : inner + 1]
                to_ref[at + 6 : at + 7] = window[k, bx + side : bx + side + 1]
        to_ref[0:bx] = total[0:bx]
        to_ref[edge_at : edge_at + 2] = total[bx : bx + 2]
        main = [jnp.zeros((half, LANES), jnp.float32) for _ in range(2)]
        ends = [jnp.zeros((1, LANES), jnp.float32) for _ in range(2)]
        for side, oy in enumerate((1, -1)):
            at = by - 1 if oy > 0 else 0
            edge = 0 if oy > 0 else by - B
            y, z = place[0, oy]
            weight = z_weight(z, half_c, same) * as_float(y == edge)
            for k in range(3):
                to = k * 2 * SIDE + side * SIDE
                for h in range(2):
                    value = shifted(z, same, k * stride + h * half * pitch + at, half, pitch, to + 64 * h)
                    main[h] = jnp.where(line_id == 2 * k + side, value * weight, main[h])
            for n, ox in enumerate((1, -1)):
                y, z = place[ox, oy]
                weight = z_weight(z, half_c, same) * as_float(y == edge)
                x = bx - 1 if ox > 0 else 0
                for k in range(3):
                    to = k * 2 * SIDE + side * SIDE
                    value = shifted(z, same, k * stride + x * pitch + at, 1, 1, to)
                    ends[n] = jnp.where(line_id == 2 * k + side, value * weight, ends[n])
        to_ref[bx:edge_at] = jnp.where(lane1 < 64, main[0], main[1])
        for n in range(2):
            to_ref[line_at + n : line_at + n + 1] = jnp.where(lane1 < 64, ends[n], 0.0)

    own = w_buf.at[iy]
    for k in range(3):
        window[k, bx + 2 : bx + 8] = jnp.zeros((6, LANES), jnp.float32)
    for load in field_loads:
        load.wait()
    columns_load.wait()
    pack(anchors[0], False, z_send)
    z_copy = pltpu.make_async_remote_copy(
        src_ref=z_send, dst_ref=z_recv, send_sem=z_sem.at[0], recv_sem=z_sem.at[1],
        device_id={"gz": 1 - iz}, device_id_type=mesh_id,
    )
    z_copy.start()
    pack(anchors[1], True, own)
    z_copy.wait()
    own[...] += z_recv[...]

    def w_copy(o):
        return y_copy(1, o, own, own)

    run(ny, [w_copy], "start")

    run(ny, [p1_copy], "wait")
    for t in range(nx):
        there = dev == (t * ny + iy) * nz + iz
        for i in range(IFACES):
            code = jnp.where(there & (box == i), far_dev[0], jnp.where(there & (box == i - 1), far_dev[1], -1))
            sy = lax.rem(lax.div(jnp.maximum(jnp.max(code), 0), nz), ny)
            at = SLOTS if i == 0 else (0 if i == SLOTS else i)
            p2_send[t, i] = p_buf[sy, at]
    p2_buf[ix] = p2_send[ix]

    def p2_copy(o):
        return x_copy(3, o, p2_send.at[x_peer(o)], p2_buf.at[ix])

    run(nx, [p2_copy], "start")

    homes = [pick(dev == (t * ny + iy) * nz + iz, home) for t in range(nx)]

    def brick_plan(t):
        here = brick == (ix * ny + t) * nz + iz
        held = [pick(here & (box == j), slot) for j in range(SLOTS)]
        low = pick(here & (box == 0), near_slot[0])
        high = pick(here & (box == SLOTS - 1), near_slot[1])
        near = [(held[j - 1] if j > 0 else low, held[j + 1] if j < SLOTS - 1 else high) for j in range(SLOTS)]
        return [jnp.maximum(n, 0) for n in held], near

    bricks = [brick_plan(t) for t in range(ny)]
    own_held, own_near = brick_plan(iy)

    run(ny, [w_copy], "wait")
    lines_load.wait()
    low_line = rem(line_id, 2) == 0
    target_home = [jnp.maximum(h, 0) for h in homes]
    target_x = [lax.div(h, ny) for h in target_home] + [ix]
    target_y = [lax.rem(h, ny) for h in target_home] + [iy]
    mixed = []
    for hy in target_y:
        before, after = jnp.maximum(hy - 1, 0), jnp.minimum(hy + 1, ny - 1)
        low_on, high_on = as_float(hy > 0), as_float(hy < ny - 1)
        for first, last in ((bx, edge_at), (line_at, line_at + 2)):
            low, high = w_buf[before, first:last] * low_on, w_buf[after, first:last] * high_on
            mixed.append(jnp.where(low_line, low, high))
        mixed.append(jnp.zeros((6, LANES), jnp.float32))
    extras = exact_right(jnp.concatenate(mixed, axis=0), lines[...])

    def assemble(n):
        hy = target_y[n]
        extra = extras[n * (half + 8) : (n + 1) * (half + 8)]
        base = w_buf[hy]
        main = (base[0:half] + extra[0:half, 0:LANES], base[half:bx] + extra[0:half, LANES : 2 * LANES])
        ends = base[edge_at : edge_at + 2] + extra[half : half + 2, 0:LANES]
        inner, outer = {}, {}
        for k in range(3):
            for side in range(2):
                at = inner_at + 2 * k + side
                first = (2 + 2 * k + side) * LANES
                from_row = 0 if side == 0 else half - 1
                inner[k, side] = base[at : at + 1] + extra[from_row : from_row + 1, first : first + LANES]
                first = (2 + 2 * k) * LANES
                outer[k, side] = base[at + 6 : at + 7] + extra[half + side : half + side + 1, first : first + LANES]
        return main, ends, inner, outer

    home_main, home_ends, home_inner, home_outer = assemble(nx)
    for t in range(nx):
        main, ends, inner, outer = assemble(t)
        d = target_x[t] - ix
        same, up_one, down_one = as_float(d == 0), as_float(d == 1), as_float(d == -1)
        e_send[t, 0:half] = main[0] * same
        e_send[t, half:bx] = main[1] * same
        e_send[t, bx : bx + 1] = ends[0:1] * up_one
        e_send[t, bx + 1 : bx + 2] = ends[1:2] * down_one
        for k in range(3):
            for side in range(2):
                at = bx + 2 + 2 * k + side
                e_send[t, at : at + 1] = inner[k, side] * (0.25 * same) + outer[k, side] * (
                    0.75 * (down_one if side else up_one)
                )
        above = ix < t
        at = bx + 8
        e_send[t, at : at + 1] = jnp.where(above, home_ends[0:1], home_ends[1:2])
        for k in range(3):
            e_send[t, at + 1 + k : at + 2 + k] = 0.75 * jnp.where(above, home_outer[k, 0], home_outer[k, 1])
        e_send[t, at + 4 : E_ROWS] = jnp.zeros((E_ROWS - at - 4, LANES), jnp.float32)
    e_buf[ix] = e_send[ix]

    def e_copy(o):
        return x_copy(4, o, e_send.at[x_peer(o)], e_buf.at[ix])

    run(nx, [e_copy], "start")

    run(nx, [f_copy, m_copy, c_copy], "wait")
    side_x = SLOTS * nz * ny
    for t in range(ny):
        held, near = bricks[t]
        for j in range(SLOTS):
            n = held[j]
            tx, s = lax.div(n, side_x), lax.rem(n, SLOTS)
            qm_send[t, j] = m_buf[tx, s]
            rim = c_buf[tx, lax.rem(s, 2)]
            flip = lax.div(s, 2) != j // 2
            rim = jnp.where(flip, pltpu.roll(rim, 64, 1), rim)
            keep = lane_f < 64 if j < 2 else lane_f >= 64
            if j < 2:
                qc_send[t, j] = rim
            else:
                qc_send[t, j % 2] = jnp.where(keep, rim, qc_send[t, j % 2])
            for side in range(2):
                other = lax.div(jnp.maximum(near[j][side], 0), side_x)
                if side == 0:
                    at = j if j > 0 else SLOTS
                else:
                    at = j + 1 if j < SLOTS - 1 else 0
                qf_send[t, 2 * j + side, 0:3] = f_buf[other, at, 0:3]
                qf_send[t, 2 * j + side, 3:4] = f_buf[tx, j + side, 3:4]
    qm_buf[iy] = qm_send[iy]
    qc_buf[iy] = qc_send[iy]
    qf_buf[iy] = qf_send[iy]

    def qm_copy(o):
        return y_copy(2, o, qm_send.at[y_peer(o)], qm_buf.at[iy])

    def qc_copy(o):
        return y_copy(3, o, qc_send.at[y_peer(o)], qc_buf.at[iy])

    def qf_copy(o):
        return y_copy(4, o, qf_send.at[y_peer(o)], qf_buf.at[iy])

    run(ny, [qf_copy, qc_copy, qm_copy], "start")

    def blended(boxes_of):
        shape = (SLOTS * F, bx + 8)
        out_line = lax.broadcasted_iota(jnp.int32, shape, 0)
        from_line = lax.broadcasted_iota(jnp.int32, shape, 1)
        boxes = jnp.full(shape, boxes_of[0], jnp.int32)
        for s in range(1, SLOTS):
            boxes = jnp.where(out_line // F == s, boxes_of[s], boxes)
        f_id = out_line % F
        center = B * boxes + f_id // 2
        other = jnp.where(f_id % 2 == 0, center - 1, center + 1)
        other = jnp.where(other < 0, bx, jnp.where(other >= bx, bx + 1, other))
        return jnp.where(from_line == center, 0.75, jnp.where(from_line == other, 0.25, 0.0))

    blend = blended([slots[s][1] for s in range(SLOTS)])
    home_blend = blended(list(range(SLOTS)))
    run(nx, [p2_copy], "wait")
    for load in (ghost_load, rim_ghost_load, rim_mean_load):
        load.wait()
    run(nx, [e_copy], "wait")
    total = e_buf[0, 0 : bx + 8]
    for t in range(1, nx):
        total += e_buf[t, 0 : bx + 8]
    along = exact_left(blend, total)
    ghosts = exact_right(along, ghost[:, 0 : 3 * F * F])
    faces = exact_right(total[bx : bx + 8], ghost[:, 3 * F * F :])
    for s in range(SLOTS):
        active, b, near = slots[s]
        cv = step_rate * visc[s]
        for k in range(3):
            ends = []
            for side in range(2):
                has, is_local, _, sx = near[side]
                far = p2_buf[sx, b + side, k : k + 1]
                outer = faces[2 + 2 * k + side : 3 + 2 * k + side]
                ends.append(jnp.where(has, far * as_float(~is_local), outer))
            edge = jnp.where(row == 0, ends[0], jnp.where(row == F - 1, ends[1], 0.0))
            at = (s * 3 + k) * F
            ghost_k = ghosts[s * F : s * F + F, k * F * F : (k + 1) * F * F]
            adv = jnp.concatenate([advs[0, at : at + F], advs[1, at : at + F]], axis=1) + cv * (ghost_k + edge)
            fine_out[k, s] = jnp.where(active, adv, 0.0)

    before = e_buf[jnp.maximum(ix - 1, 0), bx + 8 : E_ROWS] * as_float(ix > 0)
    after = e_buf[jnp.minimum(ix + 1, nx - 1), bx + 8 : E_ROWS] * as_float(ix < nx - 1)
    face_lines = []
    for k in range(3):
        for side in range(2):
            far = after if side else before
            face_lines.append(0.25 * home_inner[k, side] + far[1 + k : 2 + k])
    home_total = jnp.concatenate([*home_main, before[0:1], after[0:1], *face_lines], axis=0)
    home_along = exact_left(home_blend, home_total)
    rim_ghosts = exact_right(home_along, rim_ghost[...])
    home_faces = exact_right(home_total[bx : bx + 8], ghost[:, 3 * F * F :])
    run(ny, [qf_copy, qc_copy, qm_copy], "wait")

    def row_of(n):
        return lax.rem(lax.div(jnp.maximum(n, 0), SLOTS * nz), ny)

    x_lines = []
    for j in range(SLOTS):
        own_row = row_of(own_held[j])
        own_dev = lax.div(own_held[j], SLOTS)
        for side in range(2):
            m = own_near[j][side]
            other_dev = lax.div(jnp.maximum(m, 0), SLOTS)
            on = as_float((m < 0) | (own_dev != other_dev))
            weight = qf_buf[own_row, 2 * j + side, 3:4] * on
            for k in range(3):
                far = qf_buf[row_of(m), 2 * j + side, k : k + 1]
                x_lines.append(weight * jnp.where(m >= 0, far, home_faces[2 + 2 * k + side : 3 + 2 * k + side]))
    x_means = exact_right(jnp.concatenate(x_lines, axis=0), mean[...])
    products = []
    for j in range(SLOTS // 2):
        low = qc_buf[row_of(own_held[j]), j]
        high = qc_buf[row_of(own_held[j + 2]), j]
        rim = jnp.where(lane_f < 64, low, high)
        for k in range(3):
            low = rim_ghosts[j * F : (j + 1) * F, k * LANES : (k + 1) * LANES]
            high = rim_ghosts[(j + 2) * F : (j + 3) * F, k * LANES : (k + 1) * LANES]
            window[(3 * j + k) // 2, (3 * j + k) % 2 * F : (3 * j + k) % 2 * F + F] = rim * jnp.where(
                lane_f < 64, low, high
            )
    for n in range(3):
        products.append(window[n, pl.ds(0, F, 2)] + window[n, pl.ds(1, F, 2)])
    rim_means = exact_right(jnp.concatenate(products, axis=0), rim_mean[...])
    for j in range(SLOTS):
        own_row = row_of(own_held[j])
        for k in range(3):
            at = (3 * (j % 2) + k) * B
            low, high = rim_means[at : at + quarter], rim_means[at + quarter : at + B]
            if j < 2:
                high = pltpu.roll(high, 64, 1)
            else:
                low = pltpu.roll(low, 64, 1)
            value = qm_buf[own_row, j, k * quarter : (k + 1) * quarter] + jnp.where(lane_m < 64, low, high)
            row_m = lax.broadcasted_iota(jnp.int32, (quarter, LANES), 0)
            for side in range(2):
                n = (2 * j + side) * 3 + k
                place = (row_m == 0) & (lane_m < 64) if side == 0 else (row_m == quarter - 1) & (lane_m >= 64)
                value += jnp.where(place, x_means[n : n + 1], 0.0)
            picked[j, k * quarter : (k + 1) * quarter] = value


def final_kernel(dims, corners, slot_ref, field, picked, fine, coarse_out, fine_out, group, sems):
    nx, ny, nz, bx, by, bz = dims
    ix, iy, iz = lax.axis_index("gx"), lax.axis_index("gy"), lax.axis_index("gz")
    me = (ix * ny + iy) * nz + iz
    _, _, _, brick, place = grid_tables((bx, by, bz), ny, nz, corners, slot_ref)
    code = pick(brick == me, place)
    present = code >= 0
    code = jnp.maximum(code, 0)
    y_group = lax.div(lax.div(code, bz), B)
    z = lax.rem(code, bz)
    fine_copy = pltpu.make_async_copy(fine, fine_out, sems.at[0])
    fine_copy.start()

    def plain(g):
        return pltpu.make_async_copy(
            field.at[:, pl.ds(g * B, B)], coarse_out.at[:, pl.ds(g * B, B)], sems.at[1 + g]
        )

    def patched(g):
        return pltpu.make_async_copy(group, coarse_out.at[:, pl.ds(g * B, B)], sems.at[1 + g])

    for g in range(by // B):

        @pl.when(y_group != g)
        def _():
            plain(g).start()

    start = pl.multiple_of(y_group * B, B)
    low = lax.rem(z, LANES)
    tile = lax.div(z, LANES)
    lane = lax.broadcasted_iota(jnp.int32, (B, LANES), 1)
    eight = lane // B
    line = lax.broadcasted_iota(jnp.int32, (B, LANES), 0)
    chosen = eight % B == line
    first_half = (eight - line + 16) % 16 < B
    inside = [(lane >= low) & (lane < low + B) & (tile == t) & present for t in range(bz // LANES)]
    for j in range(SLOTS):
        for at in range(MEAN_ROWS):
            value = jnp.where(chosen, jnp.broadcast_to(picked[j, at : at + 1], (B, LANES)), 0.0)
            for step in (B, 2 * B, 4 * B):
                value += pltpu.roll(value, step, 1)
            swapped = pltpu.roll(value, 64, 1)
            k, a = at // (B // 2), at % (B // 2)
            for h in range(2):
                new = jnp.where(first_half, value, swapped) if h == 0 else jnp.where(first_half, swapped, value)
                x = k * bx + j * B + h * (B // 2) + a
                for t in range(bz // LANES):
                    old = field[x, pl.ds(start, B), t * LANES : (t + 1) * LANES]
                    group[x, :, t * LANES : (t + 1) * LANES] = jnp.where(inside[t], new, old)
    patched(y_group).start()
    for g in range(by // B):
        patched(g).wait()
    fine_copy.wait()


def on_device(coarse_field, fine_field, viscosity, corners, grid_slot, neighbors):
    nx, ny, nz = (lax.axis_size(n) for n in ("gx", "gy", "gz"))
    assert nz == 2
    bx, by, bz = coarse_field.shape[1:]
    dims = (nx, ny, nz, bx, by, bz)
    consts = matrices()
    vmem = pl.BlockSpec(memory_space=pltpu.VMEM)
    hbm = pl.BlockSpec(memory_space=pltpu.HBM)
    stay = functools.partial(pltpu.with_memory_space_constraint, memory_space=pltpu.HBM)
    grids = grid_slot.shape[0]
    f32 = jnp.float32
    dma = pltpu.SemaphoreType.DMA
    w_rows = bx + bx // 2 + 16
    planes = (IFACES, PLANE_LINES, F * F)
    means = (SLOTS, MEAN_ROWS, LANES)
    rims = (SLOTS // 2, F, LANES)
    tables_in = (corners.T, grid_slot.reshape(1, -1))
    fine_new, picked = pl.pallas_call(
        functools.partial(step_kernel, dims),
        out_shape=(
            jax.ShapeDtypeStruct(fine_field.shape, f32),
            jax.ShapeDtypeStruct((SLOTS, MEAN_ROWS, LANES), f32),
        ),
        in_specs=[hbm] * (6 + len(consts)),
        out_specs=(vmem, vmem),
        scratch_shapes=[
            pltpu.VMEM((3, grids), jnp.int32),
            pltpu.VMEM((1, grids), jnp.int32),
            pltpu.VMEM((2, grids), jnp.int32),
            pltpu.VMEM((bz // LANES, 3 * bx, by + 8, LANES), f32),
            pltpu.VMEM(fine_field.shape, f32),
            pltpu.VMEM(viscosity.shape, f32),
        ]
        + [pltpu.VMEM(c.shape, c.dtype) for c in consts]
        + [
            pltpu.VMEM(shape, f32)
            for shape in (
                (3, bx + 8, LANES),
                (w_rows, LANES),
                (w_rows, LANES),
                (ny, w_rows, LANES),
                (ny, *planes),
                (nx, *planes),
                (nx, *planes),
                (nx, *planes),
                (nx, E_ROWS, LANES),
                (nx, E_ROWS, LANES),
                (2, 3 * SLOTS * F, LANES),
                means,
                (nx, *means),
                rims,
                (nx, *rims),
                (ny, *means),
                (ny, *means),
                (ny, *rims),
                (ny, *rims),
                (ny, 2 * SLOTS, PLANE_LINES, F * F),
                (ny, 2 * SLOTS, PLANE_LINES, F * F),
            )
        ]
        + [
            dma((12 + bz // LANES,)),
            dma((2,)),
            dma((5, ny - 1)),
            dma((5, ny - 1)),
            dma((5, nx - 1)),
            dma((5, nx - 1)),
        ],
        compiler_params=pltpu.CompilerParams(collective_id=0, has_side_effects=True, vmem_limit_bytes=24 * MIB),
        name="step",
    )(
        *map(
            stay, (*tables_in, neighbors.T, coarse_field.reshape(3 * bx, by, bz), fine_field, viscosity, *consts)
        )
    )
    coarse_out, fine_out = pl.pallas_call(
        functools.partial(final_kernel, dims),
        out_shape=(
            jax.ShapeDtypeStruct((3 * bx, by, bz), f32),
            jax.ShapeDtypeStruct(fine_field.shape, f32),
        ),
        in_specs=[vmem] * 5,
        out_specs=(hbm, hbm),
        scratch_shapes=[pltpu.VMEM((3 * bx, B, bz), f32), dma((1 + by // B,))],
        compiler_params=pltpu.CompilerParams(vmem_limit_bytes=16 * MIB),
        name="final",
    )(*tables_in, coarse_field.reshape(3 * bx, by, bz), picked, fine_new)
    return fine_out, coarse_out.reshape(coarse_field.shape)


def solution(mesh):
    in_specs = (
        P(None, "gx", "gy", "gz"),
        P(None, ("gx", "gy", "gz"), None, None),
        P(("gx", "gy", "gz"), None, None),
        P(),
        P(),
        P(),
    )
    out_specs = (P(None, ("gx", "gy", "gz"), None, None), P(None, "gx", "gy", "gz"))
    return jax.shard_map(
        on_device, mesh=mesh, in_specs=in_specs, out_specs=out_specs, check_vma=False
    )
```

time: 29.1 us -> 21.1 us (0.73)
  Pallas kernels: 28.2 us -> 20.3 us
    pallas_call x1, Pallas kernels: 26.3 us -> 18.3 us  [on_device(): pl.pallas_call(functools.partial(step_kernel, dims), out_shape=(jax.Shape...]
where the time goes in v2:
time: 21.1 us; the launch traced here: 21 us
  Pallas kernels  20.3 us (96%)
  between operations  0.69 us (3%)
    pallas_call x1, Pallas kernels, on_device(): pl.pallas_call(functools.partial(step_kernel, dims), out_shape=(jax.Shape...  18.3 us
    pallas_call x1, Pallas kernels, on_device(): pl.pallas_call(functools.partial(final_kernel, dims), out_shape=(jax.Shap...  1.99 us

profile of v2, /device:TPU:0, one launch (start us, length us, event | category | flops | bytes accessed | tf_op | source)
XLA Modules:
  0.0 21.0 jit_solution(538461805839359049)
XLA Ops:
  0.6 0.0 copy-start.2
  0.6 0.0 copy-start.1
  0.7 0.0 copy-start
  0.7 18.3 %step.1 = (f32[3,4,16,256]{3,2,1,0:T(8,128)S(1)}, f32[4,12,128]{2,1,0:T(8,128)S(1)}) custom-call(s32[3,64]{1,0:T(4,128)} %bitcast.7, s32[1,64]{1,0:T(1,128)} %bitcast.9, s32[2,64]{1,0:T(2,128)} %bitcast.11, f32[96,32,256]{2,1,0:T(8,128)} %bitcast.5, f32[3,4,16,256]{3,2,1,0:T(8,128)} %fine_in.1, f32[4,16,256]{2,1,0:T(8,128)} %visc_in.1, ...), custom_call_target="tpu_custom_call" | custom-call | tf_op jit(solution)/shard_map/step/pallas_call | solution.py:740
  19.0 0.0 copy-done.2
  19.0 0.0 copy-done.1
  19.0 0.0 copy-done
  19.0 2.0 %final.1 = (f32[96,32,256]{2,1,0:T(8,128)}, f32[3,4,16,256]{3,2,1,0:T(8,128)}) custom-call(s32[3,64]{1,0:T(4,128)S(1)} %bitcast.8, s32[1,64]{1,0:T(1,128)S(1)} %bitcast.10, f32[96,32,256]{2,1,0:T(8,128)S(1)} %bitcast.6, f32[4,12,128]{2,1,0:T(8,128)S(1)} %get-tuple-element.6.picked, f32[3,4,16,256]{3,2,1,0:T(8,128)S(1)} %get-tuple-element.7.fine), custom_call_target="tpu_custom_call" | custom-call | tf_op jit(solution)/shard_map/final/pallas_call | solution.py:798
Async XLA Ops:
  0.6 18.3 %copy-start.2 = (s32[64]{0:T(128)S(1)}, s32[64]{0:T(128)}, u32[]{:S(2)}) copy-start(s32[64]{0:T(128)} %param.17) | copy-start | bytes 772
  0.6 18.3 %copy-start.1 = (s32[64,3]{0,1:T(4,128)S(1)}, s32[64,3]{0,1:T(4,128)}, u32[]{:S(2)}) copy-start(s32[64,3]{0,1:T(4,128)} %param.16) | copy-start | bytes 2308
  0.7 18.3 %copy-start = (f32[3,32,32,256]{3,2,1,0:T(8,128)S(1)}, f32[3,32,32,256]{3,2,1,0:T(8,128)}, u32[]{:S(2)}) copy-start(f32[3,32,32,256]{3,2,1,0:T(8,128)} %param.13) | copy-start | bytes 9437188

commit v3 on v2

--- a/solution.py
+++ b/solution.py
@@ -15,7 +15,8 @@
 WIDE = 4 * SIDE
 IFACES = SLOTS + 1
 PLANE_LINES = 4
-E_ROWS = 48
+FACES = 12
+E_ROWS = 44
 MEAN_ROWS = 12
 step_rate = 0.15
 MIB = 1 << 20
@@ -127,9 +128,9 @@
 def step_kernel(
     dims, corners_in, slot_in, near_in, coarse, fine_in, visc_in,
     columns_in, lines_in, ghost_in, mean_in, take_in, rim_ghost_in, rim_mean_in,
-    fine_out, picked,
-    corners, slot_ref, near_ref, field, fine, visc, columns, lines, ghost, mean, take, rim_ghost, rim_mean,
-    window, z_send, z_recv, w_buf, p_buf, f_buf, p2_send, p2_buf, e_send, e_buf,
+    fine_out, picked, field,
+    corners, slot_ref, near_ref, fine, visc, columns, lines, ghost, mean, take, rim_ghost, rim_mean,
+    window, z_send, z_recv, w_buf, p_own, f_buf, e_send, e_buf,
     advs, m_send, m_buf, c_send, c_buf, qm_send, qm_buf, qc_send, qc_buf, qf_send, qf_buf,
     local_sem, z_sem, y_send_sem, y_recv_sem, x_send_sem, x_recv_sem,
 ):
@@ -143,18 +144,20 @@
 
     pairs = [
         (corners_in, corners), (slot_in, slot_ref), (near_in, near_ref), (fine_in, fine), (visc_in, visc),
+        (mean_in, mean), (take_in, take),
     ]
     for t in range(tiles):
         pairs.append((coarse.at[:, :, t * LANES : (t + 1) * LANES], field.at[t, :, 0:by]))
     pairs += [
-        (mean_in, mean), (take_in, take), (columns_in, columns), (lines_in, lines), (ghost_in, ghost),
+        (columns_in, columns), (lines_in, lines), (ghost_in, ghost),
         (rim_ghost_in, rim_ghost), (rim_mean_in, rim_mean),
     ]
     loads = [pltpu.make_async_copy(src, dst, local_sem.at[i]) for i, (src, dst) in enumerate(pairs)]
     for load in loads:
         load.start()
-    table_loads, fine_load, visc_load, field_loads = loads[:3], loads[3], loads[4], loads[5 : 5 + tiles]
-    mean_load, take_load, columns_load, lines_load, ghost_load, rim_ghost_load, rim_mean_load = loads[5 + tiles :]
+    table_loads, field_loads = loads[:3], loads[7 : 7 + tiles]
+    fine_load, visc_load, mean_load, take_load = loads[3:7]
+    columns_load, lines_load, ghost_load, rim_ghost_load, rim_mean_load = loads[7 + tiles :]
 
     def y_peer(o):
         return lax.rem(iy + o, ny)
@@ -231,11 +234,8 @@
             m = pick(here, near_slot[side])
             n = jnp.maximum(m, 0)
             d = lax.div(n, SLOTS)
-            near.append((m >= 0, d == me, lax.rem(n, SLOTS), lax.div(d, ny * nz)))
+            near.append((m >= 0, d == me, lax.rem(n, SLOTS), lax.rem(lax.div(d, nz), ny)))
         slots.append((b >= 0, jnp.maximum(b, 0), near))
-    anchors = [
-        {(ox, oy): anchor(ox, oy, gz) for ox in (-1, 0, 1) for oy in (-1, 0, 1)} for gz in (1 - iz, iz)
-    ]
 
     fine_load.wait()
     visc_load.wait()
@@ -252,19 +252,14 @@
                 value = line(below, F - 1)
             else:
                 value = jnp.where(own_slot[i - 1] >= 0, line(below, F - 1), line(above, 0))
-            p_buf[iy, i, k : k + 1] = value
+            p_own[i, k : k + 1] = value
     pl.semaphore_wait(barrier, nx + ny - 1)
-    own_planes = p_buf.at[iy]
-
-    def p1_copy(o):
-        return y_copy(0, o, own_planes, own_planes)
 
     def f_copy(o):
-        return x_copy(0, o, own_planes, f_buf.at[ix])
-
-    run(ny, [p1_copy], "start")
+        return x_copy(0, o, p_own, f_buf.at[ix])
+
     run(nx, [f_copy], "start")
-    f_buf[ix] = p_buf[iy]
+    f_buf[ix] = p_own[...]
 
     lane = lax.broadcasted_iota(jnp.int32, (F, F * F), 1)
     row = lax.broadcasted_iota(jnp.int32, (F, F * F), 0)
@@ -317,6 +312,9 @@
     m_buf[ix] = m_send[...]
     c_buf[ix] = c_send[...]
 
+    anchors = [
+        {(ox, oy): anchor(ox, oy, gz) for ox in (-1, 0, 1) for oy in (-1, 0, 1)} for gz in (1 - iz, iz)
+    ]
     flat = field.reshape(tiles, 3 * bx * pitch, LANES)
     stride = bx * pitch
     lane1 = lax.broadcasted_iota(jnp.int32, (1, LANES), 1)
@@ -431,24 +429,9 @@
     own[...] += z_recv[...]
 
     def w_copy(o):
-        return y_copy(1, o, own, own)
+        return y_copy(0, o, own, own)
 
     run(ny, [w_copy], "start")
-
-    run(ny, [p1_copy], "wait")
-    for t in range(nx):
-        there = dev == (t * ny + iy) * nz + iz
-        for i in range(IFACES):
-            code = jnp.where(there & (box == i), far_dev[0], jnp.where(there & (box == i - 1), far_dev[1], -1))
-            sy = lax.rem(lax.div(jnp.maximum(jnp.max(code), 0), nz), ny)
-            at = SLOTS if i == 0 else (0 if i == SLOTS else i)
-            p2_send[t, i] = p_buf[sy, at]
-    p2_buf[ix] = p2_send[ix]
-
-    def p2_copy(o):
-        return x_copy(3, o, p2_send.at[x_peer(o)], p2_buf.at[ix])
-
-    run(nx, [p2_copy], "start")
 
     homes = [pick(dev == (t * ny + iy) * nz + iz, home) for t in range(nx)]
 
@@ -462,6 +445,41 @@
 
     bricks = [brick_plan(t) for t in range(ny)]
     own_held, own_near = brick_plan(iy)
+
+    side_x = SLOTS * nz * ny
+    sources = []
+    for t in range(ny):
+        there = dev == (ix * ny + t) * nz + iz
+        codes = []
+        for i in range(IFACES):
+            code = jnp.where(there & (box == i), far_dev[0], jnp.where(there & (box == i - 1), far_dev[1], -1))
+            codes.append(lax.div(jnp.maximum(jnp.max(code), 0), nz * ny))
+        sources.append(codes)
+    run(nx, [f_copy], "wait")
+    for t in range(ny):
+        held, near = bricks[t]
+        for j in range(SLOTS):
+            tx = lax.div(held[j], side_x)
+            for side in range(2):
+                other = lax.div(jnp.maximum(near[j][side], 0), side_x)
+                if side == 0:
+                    at = j if j > 0 else SLOTS
+                else:
+                    at = j + 1 if j < SLOTS - 1 else 0
+                qf_send[t, 2 * j + side, 0:3] = f_buf[other, at, 0:3]
+                qf_send[t, 2 * j + side, 3:4] = f_buf[tx, j + side, 3:4]
+        for i in range(IFACES):
+            at = SLOTS if i == 0 else (0 if i == SLOTS else i)
+            for k in range(3):
+                n = 3 * i + k
+                qf_send[t, 2 * SLOTS + n // 4, n % 4 : n % 4 + 1] = f_buf[sources[t][i], at, k : k + 1]
+        qf_send[t, FACES - 1, 3:4] = jnp.zeros((1, F * F), jnp.float32)
+    qf_buf[iy] = qf_send[iy]
+
+    def qf_copy(o):
+        return y_copy(3, o, qf_send.at[y_peer(o)], qf_buf.at[iy])
+
+    run(ny, [qf_copy], "start")
 
     run(ny, [w_copy], "wait")
     lines_load.wait()
@@ -516,18 +534,16 @@
         e_send[t, at : at + 1] = jnp.where(above, home_ends[0:1], home_ends[1:2])
         for k in range(3):
             e_send[t, at + 1 + k : at + 2 + k] = 0.75 * jnp.where(above, home_outer[k, 0], home_outer[k, 1])
-        e_send[t, at + 4 : E_ROWS] = jnp.zeros((E_ROWS - at - 4, LANES), jnp.float32)
     e_buf[ix] = e_send[ix]
 
     def e_copy(o):
-        return x_copy(4, o, e_send.at[x_peer(o)], e_buf.at[ix])
+        return x_copy(3, o, e_send.at[x_peer(o)], e_buf.at[ix])
 
     run(nx, [e_copy], "start")
 
-    run(nx, [f_copy, m_copy, c_copy], "wait")
-    side_x = SLOTS * nz * ny
+    run(nx, [m_copy, c_copy], "wait")
     for t in range(ny):
-        held, near = bricks[t]
+        held = bricks[t][0]
         for j in range(SLOTS):
             n = held[j]
             tx, s = lax.div(n, side_x), lax.rem(n, SLOTS)
@@ -540,28 +556,16 @@
                 qc_send[t, j] = rim
             else:
                 qc_send[t, j % 2] = jnp.where(keep, rim, qc_send[t, j % 2])
-            for side in range(2):
-                other = lax.div(jnp.maximum(near[j][side], 0), side_x)
-                if side == 0:
-                    at = j if j > 0 else SLOTS
-                else:
-                    at = j + 1 if j < SLOTS - 1 else 0
-                qf_send[t, 2 * j + side, 0:3] = f_buf[other, at, 0:3]
-                qf_send[t, 2 * j + side, 3:4] = f_buf[tx, j + side, 3:4]
     qm_buf[iy] = qm_send[iy]
     qc_buf[iy] = qc_send[iy]
-    qf_buf[iy] = qf_send[iy]
 
     def qm_copy(o):
-        return y_copy(2, o, qm_send.at[y_peer(o)], qm_buf.at[iy])
+        return y_copy(1, o, qm_send.at[y_peer(o)], qm_buf.at[iy])
 
     def qc_copy(o):
-        return y_copy(3, o, qc_send.at[y_peer(o)], qc_buf.at[iy])
-
-    def qf_copy(o):
-        return y_copy(4, o, qf_send.at[y_peer(o)], qf_buf.at[iy])
-
-    run(ny, [qf_copy, qc_copy, qm_copy], "start")
+        return y_copy(2, o, qc_send.at[y_peer(o)], qc_buf.at[iy])
+
+    run(ny, [qc_copy, qm_copy], "start")
 
     def blended(boxes_of):
         shape = (SLOTS * F, bx + 8)
@@ -578,10 +582,10 @@
 
     blend = blended([slots[s][1] for s in range(SLOTS)])
     home_blend = blended(list(range(SLOTS)))
-    run(nx, [p2_copy], "wait")
     for load in (ghost_load, rim_ghost_load, rim_mean_load):
         load.wait()
     run(nx, [e_copy], "wait")
+    run(ny, [qf_copy], "wait")
     total = e_buf[0, 0 : bx + 8]
     for t in range(1, nx):
         total += e_buf[t, 0 : bx + 8]
@@ -594,8 +598,9 @@
         for k in range(3):
             ends = []
             for side in range(2):
-                has, is_local, _, sx = near[side]
-                far = p2_buf[sx, b + side, k : k + 1]
+                has, is_local, _, sy = near[side]
+                n = 3 * (b + side) + k
+                far = qf_buf[sy, 2 * SLOTS + lax.div(n, 4), pl.ds(lax.rem(n, 4), 1)]
                 outer = faces[2 + 2 * k + side : 3 + 2 * k + side]
                 ends.append(jnp.where(has, far * as_float(~is_local), outer))
             edge = jnp.where(row == 0, ends[0], jnp.where(row == F - 1, ends[1], 0.0))
@@ -615,7 +620,7 @@
     home_along = exact_left(home_blend, home_total)
     rim_ghosts = exact_right(home_along, rim_ghost[...])
     home_faces = exact_right(home_total[bx : bx + 8], ghost[:, 3 * F * F :])
-    run(ny, [qf_copy, qc_copy, qm_copy], "wait")
+    run(ny, [qc_copy, qm_copy], "wait")
 
     def row_of(n):
         return lax.rem(lax.div(jnp.maximum(n, 0), SLOTS * nz), ny)
@@ -675,48 +680,50 @@
     code = jnp.maximum(code, 0)
     y_group = lax.div(lax.div(code, bz), B)
     z = lax.rem(code, bz)
-    fine_copy = pltpu.make_async_copy(fine, fine_out, sems.at[0])
-    fine_copy.start()
-
-    def plain(g):
-        return pltpu.make_async_copy(
-            field.at[:, pl.ds(g * B, B)], coarse_out.at[:, pl.ds(g * B, B)], sems.at[1 + g]
-        )
-
-    def patched(g):
-        return pltpu.make_async_copy(group, coarse_out.at[:, pl.ds(g * B, B)], sems.at[1 + g])
-
-    for g in range(by // B):
-
-        @pl.when(y_group != g)
-        def _():
-            plain(g).start()
-
-    start = pl.multiple_of(y_group * B, B)
+    tiles = bz // LANES
     low = lax.rem(z, LANES)
     tile = lax.div(z, LANES)
+    fine_copy = pltpu.make_async_copy(fine, fine_out, sems.at[0, 0])
+
+    def at(g, t):
+        return coarse_out.at[:, pl.ds(pl.multiple_of(g * B, B), B), pl.ds(pl.multiple_of(t * LANES, LANES), LANES)]
+
+    def plain(g, t):
+        return pltpu.make_async_copy(field.at[t, :, g * B : (g + 1) * B], at(g, t), sems.at[1 + g, t])
+
+    def patched(g, t):
+        return pltpu.make_async_copy(group, at(g, t), sems.at[1 + g, t])
+
+    for g in range(by // B):
+        for t in range(tiles):
+
+            @pl.when((y_group != g) | (tile != t))
+            def _():
+                plain(g, t).start()
+
+    fine_copy.start()
+    start = pl.multiple_of(y_group * B, B)
     lane = lax.broadcasted_iota(jnp.int32, (B, LANES), 1)
     eight = lane // B
     line = lax.broadcasted_iota(jnp.int32, (B, LANES), 0)
     chosen = eight % B == line
     first_half = (eight - line + 16) % 16 < B
-    inside = [(lane >= low) & (lane < low + B) & (tile == t) & present for t in range(bz // LANES)]
+    inside = (lane >= low) & (lane < low + B) & present
     for j in range(SLOTS):
-        for at in range(MEAN_ROWS):
-            value = jnp.where(chosen, jnp.broadcast_to(picked[j, at : at + 1], (B, LANES)), 0.0)
+        for row in range(MEAN_ROWS):
+            value = jnp.where(chosen, jnp.broadcast_to(picked[j, row : row + 1], (B, LANES)), 0.0)
             for step in (B, 2 * B, 4 * B):
                 value += pltpu.roll(value, step, 1)
             swapped = pltpu.roll(value, 64, 1)
-            k, a = at // (B // 2), at % (B // 2)
+            k, a = row // (B // 2), row % (B // 2)
             for h in range(2):
                 new = jnp.where(first_half, value, swapped) if h == 0 else jnp.where(first_half, swapped, value)
                 x = k * bx + j * B + h * (B // 2) + a
-                for t in range(bz // LANES):
-                    old = field[x, pl.ds(start, B), t * LANES : (t + 1) * LANES]
-                    group[x, :, t * LANES : (t + 1) * LANES] = jnp.where(inside[t], new, old)
-    patched(y_group).start()
+                group[x] = jnp.where(inside, new, field[tile, x, pl.ds(start, B)])
+    patched(y_group, tile).start()
     for g in range(by // B):
-        patched(g).wait()
+        for t in range(tiles):
+            patched(g, t).wait()
     fine_copy.wait()
 
 
@@ -737,19 +744,19 @@
     means = (SLOTS, MEAN_ROWS, LANES)
     rims = (SLOTS // 2, F, LANES)
     tables_in = (corners.T, grid_slot.reshape(1, -1))
-    fine_new, picked = pl.pallas_call(
+    fine_new, picked, field = pl.pallas_call(
         functools.partial(step_kernel, dims),
         out_shape=(
             jax.ShapeDtypeStruct(fine_field.shape, f32),
             jax.ShapeDtypeStruct((SLOTS, MEAN_ROWS, LANES), f32),
+            jax.ShapeDtypeStruct((bz // LANES, 3 * bx, by + 8, LANES), f32),
         ),
         in_specs=[hbm] * (6 + len(consts)),
-        out_specs=(vmem, vmem),
+        out_specs=(vmem, vmem, vmem),
         scratch_shapes=[
             pltpu.VMEM((3, grids), jnp.int32),
             pltpu.VMEM((1, grids), jnp.int32),
             pltpu.VMEM((2, grids), jnp.int32),
-            pltpu.VMEM((bz // LANES, 3 * bx, by + 8, LANES), f32),
             pltpu.VMEM(fine_field.shape, f32),
             pltpu.VMEM(viscosity.shape, f32),
         ]
@@ -761,9 +768,7 @@
                 (w_rows, LANES),
                 (w_rows, LANES),
                 (ny, w_rows, LANES),
-                (ny, *planes),
-                (nx, *planes),
-                (nx, *planes),
+                planes,
                 (nx, *planes),
                 (nx, E_ROWS, LANES),
                 (nx, E_ROWS, LANES),
@@ -776,17 +781,17 @@
                 (ny, *means),
                 (ny, *rims),
                 (ny, *rims),
-                (ny, 2 * SLOTS, PLANE_LINES, F * F),
-                (ny, 2 * SLOTS, PLANE_LINES, F * F),
+                (ny, FACES, PLANE_LINES, F * F),
+                (ny, FACES, PLANE_LINES, F * F),
             )
         ]
         + [
             dma((12 + bz // LANES,)),
             dma((2,)),
-            dma((5, ny - 1)),
-            dma((5, ny - 1)),
-            dma((5, nx - 1)),
-            dma((5, nx - 1)),
+            dma((4, ny - 1)),
+            dma((4, ny - 1)),
+            dma((4, nx - 1)),
+            dma((4, nx - 1)),
         ],
         compiler_params=pltpu.CompilerParams(collective_id=0, has_side_effects=True, vmem_limit_bytes=24 * MIB),
         name="step",
@@ -803,10 +808,10 @@
         ),
         in_specs=[vmem] * 5,
         out_specs=(hbm, hbm),
-        scratch_shapes=[pltpu.VMEM((3 * bx, B, bz), f32), dma((1 + by // B,))],
+        scratch_shapes=[pltpu.VMEM((3 * bx, B, LANES), f32), dma((1 + by // B, bz // LANES))],
         compiler_params=pltpu.CompilerParams(vmem_limit_bytes=16 * MIB),
         name="final",
-    )(*tables_in, coarse_field.reshape(3 * bx, by, bz), picked, fine_new)
+    )(*tables_in, field, picked, fine_new)
     return fine_out, coarse_out.reshape(coarse_field.shape)
 
 

time: 21.1 us -> 20 us (0.948)
  Pallas kernels: 20.3 us -> 19.1 us
    pallas_call x1, Pallas kernels: 18.3 us -> 17 us  [on_device(): pl.pallas_call(functools.partial(step_kernel, dims), out_shape=(jax.Shape...]
where the time goes in v3:
time: 20 us; the launch traced here: 19.8 us
  Pallas kernels  19.1 us (96%)
  between operations  0.67 us (3%)
    pallas_call x1, Pallas kernels, on_device(): pl.pallas_call(functools.partial(step_kernel, dims), out_shape=(jax.Shape...  17 us
    pallas_call x1, Pallas kernels, on_device(): pl.pallas_call(functools.partial(final_kernel, dims), out_shape=(jax.Shap...  2.1 us

profile of v3, /device:TPU:0, one launch (start us, length us, event | category | flops | bytes accessed | tf_op | source)
XLA Modules:
  0.0 19.8 jit_solution(1279859235285793270)
XLA Ops:
  0.6 0.0 copy-start.1
  0.6 0.0 copy-start
  0.7 17.0 %step.1 = (f32[3,4,16,256]{3,2,1,0:T(8,128)S(1)}, f32[4,12,128]{2,1,0:T(8,128)S(1)}, f32[2,96,40,128]{3,2,1,0:T(8,128)S(1)}) custom-call(s32[3,64]{1,0:T(4,128)} %bitcast.5, s32[1,64]{1,0:T(1,128)} %bitcast.7, s32[2,64]{1,0:T(2,128)} %bitcast.10, f32[96,32,256]{2,1,0:T(8,128)} %bitcast.9, f32[3,4,16,256]{3,2,1,0:T(8,128)} %fine_in.1, f32[4,16,256]{2,1,0:T(8,128)} %visc_in.1, ...), custom_call_target="tpu_custom_call" | custom-call | tf_op jit(solution)/shard_map/step/pallas_call | solution.py:747
  17.7 0.0 copy-done.1
  17.7 0.0 copy-done
  17.7 2.1 %final.1 = (f32[96,32,256]{2,1,0:T(8,128)}, f32[3,4,16,256]{3,2,1,0:T(8,128)}) custom-call(s32[3,64]{1,0:T(4,128)S(1)} %bitcast.6, s32[1,64]{1,0:T(1,128)S(1)} %bitcast.8, f32[2,96,40,128]{3,2,1,0:T(8,128)S(1)} %get-tuple-element.7.field, f32[4,12,128]{2,1,0:T(8,128)S(1)} %get-tuple-element.8.picked, f32[3,4,16,256]{3,2,1,0:T(8,128)S(1)} %get-tuple-element.9.fine), custom_call_target="tpu_custom_call" | custom-call | tf_op jit(solution)/shard_map/final/pallas_call | solution.py:803
Async XLA Ops:
  0.6 17.1 %copy-start.1 = (s32[64]{0:T(128)S(1)}, s32[64]{0:T(128)}, u32[]{:S(2)}) copy-start(s32[64]{0:T(128)} %param.17) | copy-start | bytes 772
  0.6 17.1 %copy-start = (s32[64,3]{0,1:T(4,128)S(1)}, s32[64,3]{0,1:T(4,128)}, u32[]{:S(2)}) copy-start(s32[64,3]{0,1:T(4,128)} %param.16) | copy-start | bytes 2308

commit v4 on v3

--- a/solution.py
+++ b/solution.py
@@ -199,6 +199,11 @@
 
         lax.fori_loop(1, count, body, 0)
 
+    def run_if(cond, count, makes):
+        @pl.when(cond)
+        def _():
+            run(count, makes, "start")
+
     for load in table_loads:
         load.wait()
     gx_, gy_, slot, brick, place = grid_tables((bx, by, bz), ny, nz, corners, slot_ref)
@@ -253,13 +258,10 @@
             else:
                 value = jnp.where(own_slot[i - 1] >= 0, line(below, F - 1), line(above, 0))
             p_own[i, k : k + 1] = value
-    pl.semaphore_wait(barrier, nx + ny - 1)
 
     def f_copy(o):
         return x_copy(0, o, p_own, f_buf.at[ix])
 
-    run(nx, [f_copy], "start")
-    f_buf[ix] = p_own[...]
 
     lane = lax.broadcasted_iota(jnp.int32, (F, F * F), 1)
     row = lax.broadcasted_iota(jnp.int32, (F, F * F), 0)
@@ -295,22 +297,12 @@
             m_send[s, k * quarter : (k + 1) * quarter] = jnp.where(
                 lane_m < 64, z[at : at + quarter], z[at + quarter : at + B]
             )
-    take_load.wait()
-    lane_f = lax.broadcasted_iota(jnp.int32, (F, LANES), 1)
-    rims = exact_right(step_rate * visc[...].reshape(SLOTS * F, F * F), take[...])
-    for s in range(SLOTS // 2):
-        low, high = rims[s * F : (s + 1) * F], rims[(s + 2) * F : (s + 3) * F]
-        c_send[s] = jnp.where(lane_f < 64, low, high)
-
     def m_copy(o):
         return x_copy(1, o, m_send, m_buf.at[ix])
 
-    def c_copy(o):
-        return x_copy(2, o, c_send, c_buf.at[ix])
-
-    run(nx, [m_copy, c_copy], "start")
-    m_buf[ix] = m_send[...]
-    c_buf[ix] = c_send[...]
+    pl.semaphore_wait(barrier, nx + ny - 1)
+    run(nx, [f_copy], "start")
+    run_if(iz == 1, nx, [m_copy])
 
     anchors = [
         {(ox, oy): anchor(ox, oy, gz) for ox in (-1, 0, 1) for oy in (-1, 0, 1)} for gz in (1 - iz, iz)
@@ -425,6 +417,20 @@
     )
     z_copy.start()
     pack(anchors[1], True, own)
+    take_load.wait()
+    lane_f = lax.broadcasted_iota(jnp.int32, (F, LANES), 1)
+    rims = exact_right(step_rate * visc[...].reshape(SLOTS * F, F * F), take[...])
+    for s in range(SLOTS // 2):
+        low, high = rims[s * F : (s + 1) * F], rims[(s + 2) * F : (s + 3) * F]
+        c_send[s] = jnp.where(lane_f < 64, low, high)
+
+    def c_copy(o):
+        return x_copy(2, o, c_send, c_buf.at[ix])
+
+    run_if(iz == 1, nx, [c_copy])
+    f_buf[ix] = p_own[...]
+    m_buf[ix] = m_send[...]
+    c_buf[ix] = c_send[...]
     z_copy.wait()
     own[...] += z_recv[...]
 
@@ -432,6 +438,7 @@
         return y_copy(0, o, own, own)
 
     run(ny, [w_copy], "start")
+    run_if(iz == 0, nx, [m_copy, c_copy])
 
     homes = [pick(dev == (t * ny + iy) * nz + iz, home) for t in range(nx)]
 
@@ -674,6 +681,8 @@
     nx, ny, nz, bx, by, bz = dims
     ix, iy, iz = lax.axis_index("gx"), lax.axis_index("gy"), lax.axis_index("gz")
     me = (ix * ny + iy) * nz + iz
+    fine_copy = pltpu.make_async_copy(fine, fine_out, sems.at[0, 0])
+    fine_copy.start()
     _, _, _, brick, place = grid_tables((bx, by, bz), ny, nz, corners, slot_ref)
     code = pick(brick == me, place)
     present = code >= 0
@@ -683,8 +692,6 @@
     tiles = bz // LANES
     low = lax.rem(z, LANES)
     tile = lax.div(z, LANES)
-    fine_copy = pltpu.make_async_copy(fine, fine_out, sems.at[0, 0])
-
     def at(g, t):
         return coarse_out.at[:, pl.ds(pl.multiple_of(g * B, B), B), pl.ds(pl.multiple_of(t * LANES, LANES), LANES)]
 
@@ -701,7 +708,6 @@
             def _():
                 plain(g, t).start()
 
-    fine_copy.start()
     start = pl.multiple_of(y_group * B, B)
     lane = lax.broadcasted_iota(jnp.int32, (B, LANES), 1)
     eight = lane // B

time: 20 us -> 19.6 us (0.980)
  Pallas kernels: 19.1 us -> 18.8 us
    pallas_call x1, Pallas kernels: 17 us -> 16.7 us  [on_device(): pl.pallas_call(functools.partial(step_kernel, dims), out_shape=(jax.Shape...]
where the time goes in v4:
time: 19.6 us; the launch traced here: 19.4 us
  Pallas kernels  18.8 us (96%)
  between operations  0.67 us (3%)
    pallas_call x1, Pallas kernels, on_device(): pl.pallas_call(functools.partial(step_kernel, dims), out_shape=(jax.Shape...  16.7 us
    pallas_call x1, Pallas kernels, on_device(): pl.pallas_call(functools.partial(final_kernel, dims), out_shape=(jax.Shap...  2.04 us

profile of v4, /device:TPU:0, one launch (start us, length us, event | category | flops | bytes accessed | tf_op | source)
XLA Modules:
  0.0 19.4 jit_solution(2927332757416718141)
XLA Ops:
  0.6 0.0 copy-start.1
  0.6 0.0 copy-start
  0.7 16.7 %step.1 = (f32[3,4,16,256]{3,2,1,0:T(8,128)S(1)}, f32[4,12,128]{2,1,0:T(8,128)S(1)}, f32[2,96,40,128]{3,2,1,0:T(8,128)S(1)}) custom-call(s32[3,64]{1,0:T(4,128)} %bitcast.5, s32[1,64]{1,0:T(1,128)} %bitcast.7, s32[2,64]{1,0:T(2,128)} %bitcast.10, f32[96,32,256]{2,1,0:T(8,128)} %bitcast.9, f32[3,4,16,256]{3,2,1,0:T(8,128)} %fine_in.1, f32[4,16,256]{2,1,0:T(8,128)} %visc_in.1, ...), custom_call_target="tpu_custom_call" | custom-call | tf_op jit(solution)/shard_map/step/pallas_call | solution.py:753
  17.4 0.0 copy-done.1
  17.4 0.0 copy-done
  17.4 2.0 %final.1 = (f32[96,32,256]{2,1,0:T(8,128)}, f32[3,4,16,256]{3,2,1,0:T(8,128)}) custom-call(s32[3,64]{1,0:T(4,128)S(1)} %bitcast.6, s32[1,64]{1,0:T(1,128)S(1)} %bitcast.8, f32[2,96,40,128]{3,2,1,0:T(8,128)S(1)} %get-tuple-element.7.field, f32[4,12,128]{2,1,0:T(8,128)S(1)} %get-tuple-element.8.picked, f32[3,4,16,256]{3,2,1,0:T(8,128)S(1)} %get-tuple-element.9.fine), custom_call_target="tpu_custom_call" | custom-call | tf_op jit(solution)/shard_map/final/pallas_call | solution.py:809
Async XLA Ops:
  0.6 16.7 %copy-start.1 = (s32[64]{0:T(128)S(1)}, s32[64]{0:T(128)}, u32[]{:S(2)}) copy-start(s32[64]{0:T(128)} %param.17) | copy-start | bytes 772
  0.6 16.7 %copy-start = (s32[64,3]{0,1:T(4,128)S(1)}, s32[64,3]{0,1:T(4,128)}, u32[]{:S(2)}) copy-start(s32[64,3]{0,1:T(4,128)} %param.16) | copy-start | bytes 2308

commit v5 on v4

--- a/solution.py
+++ b/solution.py
@@ -74,9 +74,13 @@
             take[at, half * 64 + m] = 1.0
             rim_ghost[:, :, half * 64 + m] = ghost[:, :3, at]
             rim_mean[half * 64 + m, half * 64 + (at // F // 2) * B + at % F // 2] = 0.125
+    def twice(a):
+        a = a.reshape(LANES, -1)
+        return np.concatenate([a, a], axis=0)
+
     shapes = (
-        columns.reshape(3 * LANES, LANES), lines.reshape(LANES, 8 * LANES), ghost.reshape(LANES, 4 * F * F),
-        mean, take, rim_ghost.reshape(LANES, 3 * LANES), rim_mean,
+        np.concatenate([twice(a) for a in columns], axis=0), twice(lines), twice(ghost),
+        mean, take, twice(rim_ghost), twice(rim_mean),
     )
     return tuple(jnp.asarray(a, jnp.bfloat16) for a in shapes)
 
@@ -100,6 +104,8 @@
 
 def exact_right(a, b):
     high, low = split(a)
+    if b.shape[0] == 2 * a.shape[1]:
+        return dot(jnp.concatenate([high, low], axis=1), b)
     return dot(high, b) + dot(low, b)
 
 
@@ -372,7 +378,7 @@
                 window[k, bx + n : bx + n + 1] = acc[k : k + 1]
         total = jnp.zeros((bx + 8, LANES), jnp.float32)
         for k in range(3):
-            total += exact_right(window[k], columns[k * LANES : (k + 1) * LANES])
+            total += exact_right(window[k], columns[2 * k * LANES : 2 * (k + 1) * LANES])
             for side in range(2):
                 at = inner_at + 2 * k + side
                 inner = 0 if side == 0 else bx - 1
@@ -494,19 +500,23 @@
     target_home = [jnp.maximum(h, 0) for h in homes]
     target_x = [lax.div(h, ny) for h in target_home] + [ix]
     target_y = [lax.rem(h, ny) for h in target_home] + [iy]
-    mixed = []
+    mixed, side_lines = [], []
     for hy in target_y:
         before, after = jnp.maximum(hy - 1, 0), jnp.minimum(hy + 1, ny - 1)
         low_on, high_on = as_float(hy > 0), as_float(hy < ny - 1)
         for first, last in ((bx, edge_at), (line_at, line_at + 2)):
             low, high = w_buf[before, first:last] * low_on, w_buf[after, first:last] * high_on
             mixed.append(jnp.where(low_line, low, high))
+        side_lines += [mixed[-2][0:1], mixed[-2][half - 1 : half], mixed[-1]]
         mixed.append(jnp.zeros((6, LANES), jnp.float32))
-    extras = exact_right(jnp.concatenate(mixed, axis=0), lines[...])
+    extras = exact_right(jnp.concatenate(mixed, axis=0), lines[:, 0 : 2 * LANES])
+    side_lines.append(jnp.zeros((-len(target_y) * 4 % 8, LANES), jnp.float32))
+    side_extras = exact_right(jnp.concatenate(side_lines, axis=0), lines[:, 2 * LANES :])
 
     def assemble(n):
         hy = target_y[n]
         extra = extras[n * (half + 8) : (n + 1) * (half + 8)]
+        side_extra = side_extras[4 * n : 4 * n + 4]
         base = w_buf[hy]
         main = (base[0:half] + extra[0:half, 0:LANES], base[half:bx] + extra[0:half, LANES : 2 * LANES])
         ends = base[edge_at : edge_at + 2] + extra[half : half + 2, 0:LANES]
@@ -514,11 +524,10 @@
         for k in range(3):
             for side in range(2):
                 at = inner_at + 2 * k + side
-                first = (2 + 2 * k + side) * LANES
-                from_row = 0 if side == 0 else half - 1
-                inner[k, side] = base[at : at + 1] + extra[from_row : from_row + 1, first : first + LANES]
-                first = (2 + 2 * k) * LANES
-                outer[k, side] = base[at + 6 : at + 7] + extra[half + side : half + side + 1, first : first + LANES]
+                first = (2 * k + side) * LANES
+                inner[k, side] = base[at : at + 1] + side_extra[side : side + 1, first : first + LANES]
+                first = 2 * k * LANES
+                outer[k, side] = base[at + 6 : at + 7] + side_extra[2 + side : 3 + side, first : first + LANES]
         return main, ends, inner, outer
 
     home_main, home_ends, home_inner, home_outer = assemble(nx)

time: 19.6 us -> 19.5 us (level)
  Pallas kernels: 18.8 us -> 18.6 us
where the time goes in v5:
time: 19.5 us; the launch traced here: 19.3 us
  Pallas kernels  18.6 us (95%)
  between operations  0.67 us (3%)
    pallas_call x1, Pallas kernels, on_device(): pl.pallas_call(functools.partial(step_kernel, dims), out_shape=(jax.Shape...  16.6 us
    pallas_call x1, Pallas kernels, on_device(): pl.pallas_call(functools.partial(final_kernel, dims), out_shape=(jax.Shap...  2.04 us

profile of v5, /device:TPU:0, one launch (start us, length us, event | category | flops | bytes accessed | tf_op | source)
XLA Modules:
  0.0 19.3 jit_solution(2206601315794416678)
XLA Ops:
  0.6 0.0 copy-start.1
  0.6 0.0 copy-start
  0.7 16.6 %step.1 = (f32[3,4,16,256]{3,2,1,0:T(8,128)S(1)}, f32[4,12,128]{2,1,0:T(8,128)S(1)}, f32[2,96,40,128]{3,2,1,0:T(8,128)S(1)}) custom-call(s32[3,64]{1,0:T(4,128)} %bitcast.5, s32[1,64]{1,0:T(1,128)} %bitcast.7, s32[2,64]{1,0:T(2,128)} %bitcast.10, f32[96,32,256]{2,1,0:T(8,128)} %bitcast.9, f32[3,4,16,256]{3,2,1,0:T(8,128)} %fine_in.1, f32[4,16,256]{2,1,0:T(8,128)} %visc_in.1, ...), custom_call_target="tpu_custom_call" | custom-call | tf_op jit(solution)/shard_map/step/pallas_call | solution.py:762
  17.3 0.0 copy-done.1
  17.3 0.0 copy-done
  17.3 2.0 %final.1 = (f32[96,32,256]{2,1,0:T(8,128)}, f32[3,4,16,256]{3,2,1,0:T(8,128)}) custom-call(s32[3,64]{1,0:T(4,128)S(1)} %bitcast.6, s32[1,64]{1,0:T(1,128)S(1)} %bitcast.8, f32[2,96,40,128]{3,2,1,0:T(8,128)S(1)} %get-tuple-element.7.field, f32[4,12,128]{2,1,0:T(8,128)S(1)} %get-tuple-element.8.picked, f32[3,4,16,256]{3,2,1,0:T(8,128)S(1)} %get-tuple-element.9.fine), custom_call_target="tpu_custom_call" | custom-call | tf_op jit(solution)/shard_map/final/pallas_call | solution.py:818
Async XLA Ops:
  0.6 16.6 %copy-start.1 = (s32[64]{0:T(128)S(1)}, s32[64]{0:T(128)}, u32[]{:S(2)}) copy-start(s32[64]{0:T(128)} %param.17) | copy-start | bytes 772
  0.6 16.6 %copy-start = (s32[64,3]{0,1:T(4,128)S(1)}, s32[64,3]{0,1:T(4,128)}, u32[]{:S(2)}) copy-start(s32[64,3]{0,1:T(4,128)} %param.16) | copy-start | bytes 2308
